TPU v7x, 32 devices: a whole 2x2x4 slice. The times are simulated.
32 devices in a mesh: dp: 4 (over z), tensor: 8 (over y, x, core).
Axes of the slice: x: 2, y: 2, z: 4, core: 2. Of those that a mesh axis runs over, the one named last changes fastest.
Arguments:
- master: float32 [331776, 128], P(('dp', 'tensor')), may hold values from -6 to 6
- moment: float32 [331776, 128], P(('dp', 'tensor')), may hold values from -6 to 6
- second: float32 [331776, 128], P(('dp', 'tensor')), may hold values from 0.01 to 4
- gradient: bfloat16 [331776, 128], P(('dp', 'tensor')), may hold values from -6 to 6
- source_block: int32 [331776], P(('dp', 'tensor')), may hold values from 0 to 331775, as said below
Outputs:
- master_out: float32 [331776, 128], P(('dp', 'tensor'))
- moment_out: float32 [331776, 128], P(('dp', 'tensor'))
- second_out: float32 [331776, 128], P(('dp', 'tensor'))
- weight: bfloat16 [2304, 18432], P('dp')
Inputs may be any that keep to these rules, and one draw needn't show every extreme that they name: source_block is a permutation of 0 to 331775. Among the 10368 rows of one device, at most 324 hold blocks b with the same b // 10368, and some pair of devices reaches 324.
All inputs are finite; a program needn't handle non-finite values.
Results may differ from a plain program's by a relative error of at most 0.001.
Values may be sent and summed in bfloat16 or wider, within the bound.
No kernel may reach another device: no remote copies, remote signals or barrier semaphores. Data moves between devices by JAX's collectives and lax.ppermute only.
A program may use at most 128 MiB of HBM per device.

v0:
```python
import jax
import jax.numpy as jnp
from jax import lax
from jax.sharding import PartitionSpec as P

FF_WIN = 18432


decay_one = 0.9
decay_two = 0.95
learn_rate = 0.01
weight_decay = 0.1
epsilon = 1e-08
correct_one = 1.0 - 0.9**10
correct_two = 1.0 - 0.95**10


def adam_step(master, moment, second, grad_vals):
    moment_new = decay_one * moment + (1.0 - decay_one) * grad_vals
    second_new = decay_two * second + (1.0 - decay_two) * grad_vals * grad_vals
    ratio = moment_new / correct_one / (jnp.sqrt(second_new / correct_two) + epsilon)
    master_new = master - learn_rate * (ratio + weight_decay * master)
    return (master_new, moment_new, second_new)


def per_device(master, moment, second, gradient, source_block):
    rows_dev = master.shape[0]
    n_dp = lax.axis_size("dp")
    n_tensor = lax.axis_size("tensor")
    devices = n_dp * n_tensor
    capacity = (rows_dev + devices - 1) // devices
    target = source_block // rows_dev
    dest_slot = source_block % rows_dev
    matches = (target[:, None] == jnp.arange(devices, dtype=jnp.int32)[None, :]).astype(jnp.int32)
    counts = jnp.sum(matches, axis=0)
    starts = jnp.cumsum(counts) - counts
    ordering = jnp.argsort(target, stable=True)
    bucket_pos = jnp.arange(capacity, dtype=jnp.int32)
    filled = bucket_pos[None, :] < counts[:, None]
    chosen = jnp.where(filled, starts[:, None] + bucket_pos[None, :], 0)
    source_rows = ordering[chosen]
    packed = tuple(
        (
            jnp.where(filled[:, :, None], state[source_rows], 0.0)
            for state in (master, moment, second)
        )
    )
    slot_ids = jnp.where(filled, dest_slot[source_rows].astype(jnp.float32), -1.0)
    packed = packed + (slot_ids,)
    arrived = lax.all_to_all(packed, ("dp", "tensor"), split_axis=0, concat_axis=0, tiled=True)
    slot_flat = arrived[3].reshape(-1)
    total_rows = slot_flat.shape[0]
    sort_keys = jnp.where(
        slot_flat >= 0.0,
        slot_flat.astype(jnp.int32),
        rows_dev + jnp.arange(total_rows, dtype=jnp.int32),
    )
    placing = jnp.argsort(sort_keys)[:rows_dev]
    arranged = tuple((state.reshape(-1, 128)[placing] for state in arrived[:3]))
    master_out, moment_out, second_out = adam_step(
        arranged[0], arranged[1], arranged[2], gradient.astype(jnp.float32)
    )
    local_rows = master_out.astype(jnp.bfloat16).reshape(rows_dev * 128 // FF_WIN, FF_WIN)
    weight = lax.all_gather(local_rows, "tensor", axis=0, tiled=True)
    return (master_out, moment_out, second_out, weight)


def solution(mesh):
    in_specs = (
        P(("dp", "tensor"), None),
        P(("dp", "tensor"), None),
        P(("dp", "tensor"), None),
        P(("dp", "tensor"), None),
        P(("dp", "tensor")),
    )
    out_specs = (
        P(("dp", "tensor"), None),
        P(("dp", "tensor"), None),
        P(("dp", "tensor"), None),
        P("dp", None),
    )
    return jax.shard_map(
        per_device, mesh=mesh, in_specs=in_specs, out_specs=out_specs, check_vma=False
    )
```

profile of v0, /device:TPU:0, one launch (start us, length us, event | category | flops | bytes accessed | tf_op | source)
XLA Modules:
  0.0 775.4 jit_solution(17702482704165097091)
XLA Ops:
  8.2 8.2 %sort.34 = (s32[10368]{0:T(1024)}, s32[10368]{0:T(1024)S(1)}) sort(s32[10368]{0:T(1024)S(1)} %get-tuple-element.13, s32[10368]{0:T(1024)S(1)} %iota.31), dimensions={0}, to_apply=%region_1.2 | sort | flops 145152 | bytes 165888 | tf_op jit(solution)/shard_map/jit(argsort)/sort | solution.py:37
  17.0 53.6 %gather_fusion = s32[10368]{0:T(1024)S(1)} fusion(s32[10368]{0:T(1024)S(1)} %get-tuple-element.6, s32[11264]{0:T(1024)S(1)} %pad_clamp_fusion.2), kind=kCustom, calls=%fused_computation | custom fusion | bytes 124416 | tf_op jit(solution)/shard_map/gather | solution.py:41
  70.9 53.6 %gather_fusion.2 = s32[10368]{0:T(1024)S(1)} fusion(s32[10368]{0:T(1024)S(1)} %get-tuple-element.12, s32[11264]{0:T(1024)S(1)} %pad_clamp_fusion.1), kind=kCustom, calls=%fused_computation.2 | custom fusion | bytes 124416 | tf_op jit(solution)/shard_map/gather | solution.py:48
  125.4 7.3 all-to-all-start.1
  132.8 22.5 %gather_fusion.6 = f32[10368,128]{1,0:T(8,128)} fusion(f32[10368,128]{1,0:T(8,128)} %param.7, s32[11264]{0:T(1024)S(1)} %pad_clamp_fusion.1), kind=kCustom, calls=%fused_computation.6 | custom fusion | bytes 10658304 | tf_op jit(solution)/shard_map/gather | solution.py:44
  155.3 5.4 reshape.248
  160.7 22.5 %gather_fusion.4 = f32[10368,128]{1,0:T(8,128)} fusion(f32[10368,128]{1,0:T(8,128)} %param.6, s32[11264]{0:T(1024)S(1)} %pad_clamp_fusion.1), kind=kCustom, calls=%fused_computation.4 | custom fusion | bytes 10658304 | tf_op jit(solution)/shard_map/gather | solution.py:44
  183.2 5.4 reshape.232
  188.6 22.5 %gather_fusion.1 = f32[10368,128]{1,0:T(8,128)} fusion(f32[10368,128]{1,0:T(8,128)} %param.5, s32[11264]{0:T(1024)S(1)} %pad_clamp_fusion.1), kind=kCustom, calls=%fused_computation.1 | custom fusion | bytes 10658304 | tf_op jit(solution)/shard_map/gather | solution.py:44
  211.1 5.4 reshape.208
  216.4 11.4 %broadcast_select_fusion = (f32[32,324,128]{2,1,0:T(8,128)}, f32[32,324,128]{2,1,0:T(8,128)}, f32[32,324,128]{2,1,0:T(8,128)}) fusion(f32[32,324,128]{2,1,0:T(8,128)} %reshape.248, pred[32,324]{1,0:T(8,128)(4,1)S(1)} %iota_compare_fusion.2, f32[32,324,128]{2,1,0:T(8,128)} %reshape.232, f32[32,324,128]{2,1,0:T(8,128)} %reshape.208), kind=kLoop, calls=%fused_computation.13 | loop fusion | flops 3981312 | bytes 31860864 | tf_op jit(solution)/shard_map/jit(_where)/select_n | solution.py:44
  227.9 126.5 %all_to_all.21 = f32[32,324,128]{2,1,0:T(8,128)} all-to-all(f32[32,324,128]{2,1,0:T(8,128)} %get-tuple-element.14), channel_id=1, replica_groups=mesh['dp'=4,'tensor'=8] {'dp','tensor'}, dimensions={0} | all-to-all | bytes 10616832 | tf_op jit(solution)/shard_map/all_to_all | solution.py:50
  354.3 123.0 %all_to_all.22 = f32[32,324,128]{2,1,0:T(8,128)} all-to-all(f32[32,324,128]{2,1,0:T(8,128)S(1)} %copy-done), channel_id=1, replica_groups=mesh['dp'=4,'tensor'=8] {'dp','tensor'}, dimensions={0} | all-to-all | bytes 10616832 | tf_op jit(solution)/shard_map/all_to_all | solution.py:50
  481.7 8.2 %sort.35 = (s32[10368]{0:T(1024)}, s32[10368]{0:T(1024)S(1)}) sort(s32[10368]{0:T(1024)S(1)} %add_select_fusion.2, s32[10368]{0:T(1024)S(1)} %iota.33), dimensions={0}, to_apply=%region_3.4 | sort | flops 145152 | bytes 165888 | tf_op jit(solution)/shard_map/jit(argsort)/sort | solution.py:58
  490.0 5.4 reshape.197
  495.4 22.5 %gather_fusion.7 = f32[10368,128]{1,0:T(8,128)} fusion(f32[10368,128]{1,0:T(8,128)} %reshape.197, s32[11264]{0:T(1024)S(1)} %pad_clamp_fusion), kind=kCustom, calls=%fused_computation.7 | custom fusion | bytes 10658304 | tf_op jit(solution)/shard_map/gather | solution.py:59
  517.9 5.4 reshape.196
  523.3 22.5 %gather_fusion.5 = f32[10368,128]{1,0:T(8,128)} fusion(f32[10368,128]{1,0:T(8,128)} %reshape.196, s32[11264]{0:T(1024)S(1)} %pad_clamp_fusion), kind=kCustom, calls=%fused_computation.5 | custom fusion | bytes 10658304 | tf_op jit(solution)/shard_map/gather | solution.py:59
  545.8 54.5 %all-to-all-done = f32[32,324,128]{2,1,0:T(8,128)} async-done(((f32[32,324,128]{2,1,0:T(8,128)}), f32[32,324,128]{2,1,0:T(8,128)}, u32[]{:S(2)}, u32[]{:S(2)}) %all-to-all-start) | async-done | bytes 5308448 | tf_op jit(solution)/shard_map/all_to_all | solution.py:50
  600.3 5.4 reshape.195
  605.6 22.5 %gather_fusion.3 = f32[10368,128]{1,0:T(8,128)} fusion(f32[10368,128]{1,0:T(8,128)} %reshape.195, s32[11264]{0:T(1024)S(1)} %pad_clamp_fusion), kind=kCustom, calls=%fused_computation.3 | custom fusion | bytes 10658304 | tf_op jit(solution)/shard_map/gather | solution.py:59
  628.1 12.7 %fusion.3 = (bf16[10368,128]{1,0:T(8,128)(2,1)S(1)}, f32[10368,128]{1,0:T(8,128)}, f32[10368,128]{1,0:T(8,128)}, f32[10368,128]{1,0:T(8,128)}) fusion(f32[10368,128]{1,0:T(8,128)} %gather_fusion.3, bf16[10368,128]{1,0:T(8,128)(2,1)} %param.8, f32[10368,128]{1,0:T(8,128)} %gather_fusion.5, f32[10368,128]{1,0:T(8,128)} %gather_fusion.7), kind=kLoop, calls=%fused_computation.35 | loop fusion | flops 22560768 | bytes 37158912 | tf_op jit(solution)/shard_map/convert_element_type | solution.py:63
  643.5 107.8 %all-gather.2.cloned.1.call-done = bf16[576,18432]{1,0:T(8,128)(2,1)} async-done(((bf16[72,18432]{1,0:T(8,128)(2,1)}), bf16[576,18432]{1,0:T(8,128)(2,1)}) %all-gather.2.cloned.1.call-update) | async-done | bytes 21233680 | tf_op jit(solution)/shard_map/all_gather | solution.py:64
  751.2 17.3 %copy.14 = bf16[576,18432]{1,0:T(8,128)(2,1)} copy(bf16[576,18432]{1,0:T(8,128)(2,1)} %all-gather.2.cloned.1.call-done) | data formatting | bytes 42467328
  (33 shorter events, 9.9 us)
Async XLA Ops:
  125.4 102.5 %all-to-all-start.1 = ((f32[32,1,324]{2,1,0:T(1,128)}), f32[32,1,324]{2,1,0:T(1,128)S(1)}, u32[]{:S(2)}, u32[]{:S(2)}) async-start(f32[32,1,324]{2,1,0:T(1,128)} %compare_select_fusion), calls=%async_computation.1 | async-start | bytes 98304 | tf_op jit(solution)/shard_map/all_to_all | solution.py:50
  227.9 126.5 %copy-start = (f32[32,324,128]{2,1,0:T(8,128)S(1)}, f32[32,324,128]{2,1,0:T(8,128)}, u32[]{:S(2)}) copy-start(f32[32,324,128]{2,1,0:T(8,128)} %get-tuple-element.15) | copy-start | bytes 15925252
  477.3 123.0 %all-to-all-start = ((f32[32,324,128]{2,1,0:T(8,128)}), f32[32,324,128]{2,1,0:T(8,128)}, u32[]{:S(2)}, u32[]{:S(2)}) async-start(f32[32,324,128]{2,1,0:T(8,128)} %get-tuple-element.16), calls=%async_computation | async-start | bytes 10747904 | tf_op jit(solution)/shard_map/all_to_all | solution.py:50
  480.9 270.3 %all-gather.2.cloned.1.call-start = ((), (), s32[]{:S(2)}) async-start(), calls=%async_computation.4 | async-start | bytes 23887872 | tf_op jit(solution)/shard_map/all_gather | solution.py:64
Sparse Core Ops, SparseCore 0:
  643.6 107.6 all-gather.1
where the time goes:
time: 777 us; the launch traced here: 775 us
  local copies, waits for them, and re-layouts  295 us (38%)
  blocking collectives  249 us (32%)
  waiting for transfers between devices  162 us (21%)
  other arithmetic  43.1 us (6%)
  between operations  14.2 us (2%)
  starting transfers between devices  11.1 us (1%)
    all_to_all x2, blocking collectives, per_device(): lax.all_to_all(packed, ('dp', 'tensor'), split_axis=0, concat_axis=0, til...  249 us
    all_gather x1, waiting for transfers between devices, per_device(): weight = lax.all_gather(local_rows, 'tensor', axis=0, tiled=True)  108 us
    gather x6, local copies, waits for them, and re-layouts, per_device(): state[source_rows]  83.7 us
    gather x3, local copies, waits for them, and re-layouts, per_device(): arranged = tuple((state.reshape(-1, 128)[placing] for state in arrived[:3]))  67.5 us
    all_to_all x2, waiting for transfers between devices, per_device(): lax.all_to_all(packed, ('dp', 'tensor'), split_axis=0, concat_axis=0, til...  54.5 us
    gather x2, local copies, waits for them, and re-layouts, per_device(): source_rows = ordering[chosen]  53.7 us
    gather x1, local copies, waits for them, and re-layouts, per_device(): dest_slot[source_rows].astype(jnp.float32)  53.6 us
    unnamed x3, local copies, waits for them, and re-layouts  17.4 us
  transfers between devices with their start and end apart: 3, of which 2 were waited for; matrix products, arithmetic and copies ran while one was open for 21% of the time, Pallas kernels for 0%

commit v1 on v0

v1 whole, which is shorter than its diff:
```python
import functools
import math

import jax
import jax.numpy as jnp
from jax import lax
from jax.experimental import pallas as pl
from jax.experimental.pallas import tpu as pltpu
from jax.sharding import PartitionSpec as P

FF_WIN = 18432
LANES = 128
HALF = 64
QUARTER = 32

decay_one = 0.9
decay_two = 0.95
learn_rate = 0.01
weight_decay = 0.1
epsilon = 1e-08
correct_one = 1.0 - 0.9**10
correct_two = 1.0 - 0.95**10

STATE_TOP = 6.0
MASTER_INV = 2.0**12
MOMENT_INV = 2.0**20
MASTER_STEPS = 32767.0 / math.log2(1.0 + STATE_TOP * MASTER_INV)
MOMENT_STEPS = 32767.0 / math.log2(1.0 + STATE_TOP * MOMENT_INV)
SECOND_STEPS = 65535.0 / 2.0


def log_code(x, inverse_scale, steps):
    level = jnp.log2(1.0 + jnp.abs(x) * inverse_scale) * steps
    code = jnp.minimum(level + 0.5, 32767.0).astype(jnp.int32)
    return jnp.where(x < 0.0, -code, code)


def log_value(code, inverse_scale, steps):
    level = jnp.abs(code).astype(jnp.float32) * (1.0 / steps)
    size = (jnp.exp2(level) - 1.0) * (1.0 / inverse_scale)
    return jnp.where(code < 0, -size, size)


def second_code(x):
    return jnp.minimum(jnp.sqrt(x) * SECOND_STEPS + 0.5, 65535.0).astype(jnp.int32)


def second_value(code):
    root = code.astype(jnp.float32) * (1.0 / SECOND_STEPS)
    return root * root


def adam_step(master, moment, second, grad_vals):
    moment_new = decay_one * moment + (1.0 - decay_one) * grad_vals
    second_new = decay_two * second + (1.0 - decay_two) * grad_vals * grad_vals
    ratio = (moment_new * (1.0 / correct_one)) / (
        jnp.sqrt(second_new * (1.0 / correct_two)) + epsilon
    )
    master_new = master - learn_rate * (ratio + weight_decay * master)
    return (master_new, moment_new, second_new)


def round_up(value, step):
    return (value + step - 1) // step * step


class Sizes:
    def __init__(self, rows, devices, n_tensor):
        self.rows = rows
        self.devices = devices
        self.n_tensor = n_tensor
        self.cap = (rows + devices - 1) // devices
        self.groups = (self.cap + 3) // 4
        self.main = self.groups // 8 * 8
        self.tail = self.groups - self.main
        self.stride = round_up(4 * self.groups, 8)
        self.slot_rows = (self.stride + LANES - 1) // LANES
        words = 3 * self.groups
        if words % 8 + self.slot_rows > 8:
            words = round_up(words, 8)
        self.slot_at = words
        self.piece = round_up(words + self.slot_rows, 8)
        self.slot_tile = self.slot_at // 8
        self.seg = math.gcd(rows, LANES)
        self.tiles = next(n for n in (9, 8, 6, 4, 3, 2, 1) if rows % (8 * n) == 0)
        self.tile_rows = rows // self.tiles
        self.dests = next(n for n in (4, 2, 1) if devices % n == 0)
        self.w_rows = rows * LANES // FF_WIN
        self.w_blocks = FF_WIN // LANES
        self.w_tile = 8 if self.w_rows % 8 == 0 else self.w_rows
        self.w_tiles = self.w_rows // self.w_tile
        assert self.stride * devices < 65536 and rows < 32768 and self.seg % 8 == 0
        assert self.piece - 8 * self.slot_tile == 8 and self.w_blocks % 2 == 0


def index_kernel(sz, block_ref, meta_ref):
    n, seg = block_ref.shape
    block = block_ref[...]
    target = ((block.astype(jnp.float32) + 0.5) * (1.0 / sz.rows)).astype(jnp.int32)
    slot = block - target * sz.rows
    at = lax.broadcasted_iota(jnp.int32, (seg, 2 * seg), 0)
    to = lax.broadcasted_iota(jnp.int32, (seg, 2 * seg), 1)
    ahead = ((at < to) | (to >= seg)).astype(jnp.float32).astype(jnp.bfloat16)
    row = lax.broadcasted_iota(jnp.int32, (n, n), 0)
    col = lax.broadcasted_iota(jnp.int32, (n, n), 1)
    above = (col < row).astype(jnp.float32).astype(jnp.bfloat16)

    def body(step, rank):
        for u in range(8):
            hit = target == step * 8 + u
            ones = hit.astype(jnp.float32).astype(jnp.bfloat16)
            sums = jnp.dot(ones, ahead, preferred_element_type=jnp.float32)
            before = jnp.dot(
                above, sums[:, seg:].astype(jnp.bfloat16), preferred_element_type=jnp.float32
            )
            rank = rank + jnp.where(hit, sums[:, :seg] + before, 0.0)
        return rank

    rank = lax.fori_loop(0, (sz.devices + 7) // 8, body, jnp.zeros((n, seg), jnp.float32))
    meta_ref[...] = (slot << 16) | (target * sz.stride + rank.astype(jnp.int32))


def lane_of(shape):
    return lax.broadcasted_iota(jnp.int32, shape, 1)


def pack_kernel(sz, meta, master, moment, second, out0, out1, rows_w, rows_s, code_w, code_s):
    step = pl.program_id(0)

    @pl.when(step == 0)
    def _():
        def fill(i, carry):
            rows_s[pl.ds(pl.multiple_of(i * 8, 8), 8), :] = jnp.full(
                (8, LANES), sz.rows << 16, jnp.int32
            )
            return carry

        lax.fori_loop(0, sz.stride * sz.devices // 8, fill, 0)

    @pl.when(step < sz.tiles)
    def _():
        code_m = log_code(master[...], MASTER_INV, MASTER_STEPS)
        code_v = log_code(moment[...], MOMENT_INV, MOMENT_STEPS)
        code_w[...] = (code_m << 16) | (code_v & 0xFFFF)
        code_s[...] = second_code(second[...])

        def body(i, carry):
            first = step * sz.tile_rows + i * 8
            line, at = first // sz.seg, first % sz.seg
            words = [code_w[pl.ds(i * 8 + u, 1), :] for u in range(8)]
            seconds = [code_s[pl.ds(i * 8 + u, 1), :] for u in range(8)]
            for u in range(8):
                m = meta[line, at + u]
                to = m & 0xFFFF
                rows_w[pl.ds(to, 1), :] = words[u]
                rows_s[pl.ds(to, 1), :] = seconds[u] | ((m >> 16) << 16)
            return carry

        lax.fori_loop(0, sz.tile_rows // 8, body, 0)

    @pl.when(step >= sz.tiles)
    def _():
        def one(dd, carry):
            base = pl.multiple_of(((step - sz.tiles) * sz.dests + dd) * sz.stride, 8)

            def group(at, n):
                lane = lane_of((n, LANES))
                low = lane < HALF
                w = [rows_w[pl.ds(base + 4 * at + q, n, stride=4), :] for q in range(4)]
                pairs = []
                for q in range(4):
                    s = rows_s[pl.ds(base + 4 * at + q, n, stride=4), :] & 0xFFFF
                    pairs.append(s | (pltpu.roll(s, LANES - QUARTER, 1) << 16))
                r = [pltpu.roll(x, HALF, 1) for x in w]
                first = (jnp.where(low, w[0], r[1]), jnp.where(low, w[2], r[3]))
                other = (jnp.where(low, r[0], w[1]), jnp.where(low, r[2], w[3]))
                both = []
                for h in range(2):
                    joined = None
                    for q in range(4):
                        shift = (QUARTER * q - HALF * h) % LANES
                        x = pltpu.roll(pairs[q], shift, 1) if shift else pairs[q]
                        joined = x if q == 0 else jnp.where(lane < QUARTER * q, joined, x)
                    both.append(joined)
                return (first + (both[0],), other + (both[1],))

            for t in range(sz.main // 8):
                a, b = group(8 * t, 8)
                for p in range(3):
                    out0[dd, p * sz.main + 8 * t : p * sz.main + 8 * t + 8, :] = a[p]
                    out1[dd, p * sz.main + 8 * t : p * sz.main + 8 * t + 8, :] = b[p]
            if sz.tail:
                a, b = group(sz.main, sz.tail)
                for p in range(3):
                    at = 3 * sz.main + p * sz.tail
                    out0[dd, at : at + sz.tail, :] = a[p]
                    out1[dd, at : at + sz.tail, :] = b[p]
            for g in range(sz.slot_rows):
                n = min(LANES, sz.stride - g * LANES)
                slots = rows_s[pl.ds(base + g * LANES, n), :] >> 16
                row = lax.broadcasted_iota(jnp.int32, (n, LANES), 0)
                line = jnp.sum(
                    jnp.where(row == lane_of((n, LANES)), slots, 0), axis=0, keepdims=True
                )
                at = sz.slot_at + g
                out0[dd, at : at + 1, :] = line
                out1[dd, at : at + 1, :] = line
            return carry

        lax.fori_loop(0, sz.dests, one, 0)


def decode_pair(even, odd):
    lane = lane_of(even.shape)
    word = jnp.where(lane < HALF, even, pltpu.roll(odd, HALF, 1))
    low = jnp.where(lane < HALF, pltpu.roll(even, HALF, 1), odd) & 0xFFFF
    high = lax.shift_right_logical(
        jnp.where(
            lane < HALF, pltpu.roll(even, LANES - QUARTER, 1), pltpu.roll(odd, QUARTER, 1)
        ),
        16,
    )
    second = second_value(jnp.where((lane & QUARTER) == 0, low, high))
    master = log_value(word >> 16, MASTER_INV, MASTER_STEPS)
    moment = log_value((word << 16) >> 16, MOMENT_INV, MOMENT_STEPS)
    return master, moment, second


def place_kernel(sz, half, slots, words, grad, weight, kept, rows, line, grad_f32):
    step = pl.program_id(0)
    sources = sz.devices // sz.dests

    @pl.when(step < sources)
    def _():
        def one(s, carry):
            def group(at, n, x0, x1, x2):
                low = lane_of((n, LANES)) < HALF
                parts = (
                    jnp.where(low, x0, pltpu.roll(x2, HALF, 1)),
                    jnp.where(low, pltpu.roll(x0, HALF, 1), pltpu.roll(x2, QUARTER, 1)),
                    jnp.where(low, x1, x2),
                    jnp.where(low, pltpu.roll(x1, HALF, 1), pltpu.roll(x2, LANES - QUARTER, 1)),
                )
                for q in range(4):
                    line[pl.ds(4 * at + q, n, stride=4), :] = parts[q]

            for t in range(sz.main // 8):
                x = [
                    words[s, p * sz.main + 8 * t : p * sz.main + 8 * t + 8, :] for p in range(3)
                ]
                group(8 * t, 8, *x)
            if sz.tail:
                at = 3 * sz.main
                x = [words[s, at + p * sz.tail : at + (p + 1) * sz.tail, :] for p in range(3)]
                group(sz.main, sz.tail, *x)

            unroll = next(n for n in (3, 2, 1) if sz.groups % n == 0) * 4

            def body(i, carry):
                values = [line[pl.ds(i * unroll + u, 1), :] for u in range(unroll)]
                for u in range(unroll):
                    j = i * unroll + u
                    to = slots[s, sz.slot_at % 8 + j // LANES, j % LANES]
                    rows[pl.ds(to, 1), :] = values[u]
                return carry

            lax.fori_loop(0, 4 * sz.groups // unroll, body, 0)
            return carry

        lax.fori_loop(0, sz.dests, one, 0)

    @pl.when(step >= sources)
    def _():
        count = sz.w_tile * sz.w_blocks
        base = pl.multiple_of((step - sources) * count, 8)
        kept[...] = rows[pl.ds(base, count), :]
        grad_f32[...] = grad[...].astype(jnp.float32)
        low = lane_of((sz.w_tile, LANES)) < HALF
        unroll = next(n for n in (4, 3, 2, 1) if (sz.w_blocks // 2) % n == 0)

        def body(i, carry):
            for u in range(unroll):
                c = i * unroll + u
                even = rows[pl.ds(base + 2 * c, sz.w_tile, stride=sz.w_blocks), :]
                odd = rows[pl.ds(base + 2 * c + 1, sz.w_tile, stride=sz.w_blocks), :]
                g_even = grad_f32[pl.ds(2 * c, sz.w_tile, stride=sz.w_blocks), :]
                g_odd = grad_f32[pl.ds(2 * c + 1, sz.w_tile, stride=sz.w_blocks), :]
                if half == 0:
                    g_odd = pltpu.roll(g_odd, HALF, 1)
                else:
                    g_even = pltpu.roll(g_even, HALF, 1)
                master, moment, second = decode_pair(even, odd)
                new, _, _ = adam_step(master, moment, second, jnp.where(low, g_even, g_odd))
                weight[:, pl.ds(pl.multiple_of(c * LANES, LANES), LANES)] = new.astype(
                    jnp.bfloat16
                )
            return carry

        lax.fori_loop(0, sz.w_blocks // 2 // unroll, body, 0)


def state_kernel(rows0, rows1, grad, master_out, moment_out, second_out):
    n = rows0.shape[0]

    def body(i, carry):
        at = pl.ds(pl.multiple_of(i * 16, 16), 16)
        master, moment, second = decode_pair(rows0[at, :], rows1[at, :])
        new = adam_step(master, moment, second, grad[at, :].astype(jnp.float32))
        master_out[at, :], moment_out[at, :], second_out[at, :] = new
        return carry

    lax.fori_loop(0, n // 16, body, 0)


def join_kernel(first, other, weight):
    blocks = first.shape[1] // LANES
    low = lane_of((first.shape[0], LANES)) < HALF

    def body(c, carry):
        at = pl.ds(pl.multiple_of(c * LANES, LANES), LANES)
        a = first[:, at].astype(jnp.float32)
        b = other[:, at].astype(jnp.float32)
        even = jnp.where(low, a, pltpu.roll(b, HALF, 1))
        odd = jnp.where(low, pltpu.roll(a, HALF, 1), b)
        to = pl.multiple_of(c * 2 * LANES, 2 * LANES)
        weight[:, pl.ds(to, LANES)] = even.astype(jnp.bfloat16)
        weight[:, pl.ds(pl.multiple_of(to + LANES, LANES), LANES)] = odd.astype(jnp.bfloat16)
        return carry

    lax.fori_loop(0, blocks, body, 0)


def index_call(sz, source_block):
    shape = (sz.rows // sz.seg, sz.seg)
    return pl.pallas_call(
        functools.partial(index_kernel, sz),
        out_shape=jax.ShapeDtypeStruct(shape, jnp.int32),
        name="bucket_index",
    )(source_block.reshape(shape))


def pack_call(sz, meta, master, moment, second):
    tile = pl.BlockSpec((sz.tile_rows, LANES), lambda i: (jnp.minimum(i, sz.tiles - 1), 0))
    piece = pl.BlockSpec(
        (sz.dests, sz.piece, LANES), lambda i: (jnp.maximum(i - sz.tiles, 0), 0, 0)
    )
    total = sz.stride * sz.devices
    return pl.pallas_call(
        functools.partial(pack_kernel, sz),
        grid=(sz.tiles + sz.devices // sz.dests,),
        in_specs=[pl.BlockSpec(memory_space=pltpu.SMEM), tile, tile, tile],
        out_specs=[piece, piece],
        out_shape=[jax.ShapeDtypeStruct((sz.devices, sz.piece, LANES), jnp.int32)] * 2,
        scratch_shapes=[
            pltpu.VMEM((total, LANES), jnp.int32),
            pltpu.VMEM((total, LANES), jnp.int32),
            pltpu.VMEM((sz.tile_rows, LANES), jnp.int32),
            pltpu.VMEM((sz.tile_rows, LANES), jnp.int32),
        ],
        name="pack_rows",
    )(meta, master, moment, second)


def place_call(sz, half, words, gradient):
    sources = sz.devices // sz.dests
    count = sz.w_tile * sz.w_blocks
    early = lambda i: jnp.minimum(i, sources - 1)
    late = lambda i: jnp.maximum(i - sources, 0)
    return pl.pallas_call(
        functools.partial(place_kernel, sz, half),
        grid=(sources + sz.w_tiles,),
        in_specs=[
            pl.BlockSpec(
                (sz.dests, 8, LANES),
                lambda i: (early(i), sz.slot_tile, 0),
                memory_space=pltpu.SMEM,
            ),
            pl.BlockSpec((sz.dests, sz.piece, LANES), lambda i: (early(i), 0, 0)),
            pl.BlockSpec((count, LANES), lambda i: (late(i), 0)),
        ],
        out_specs=[
            pl.BlockSpec((sz.w_tile, FF_WIN // 2), lambda i: (late(i), 0)),
            pl.BlockSpec((count, LANES), lambda i: (late(i), 0)),
        ],
        out_shape=[
            jax.ShapeDtypeStruct((sz.w_rows, FF_WIN // 2), jnp.bfloat16),
            jax.ShapeDtypeStruct((sz.rows, LANES), jnp.int32),
        ],
        scratch_shapes=[
            pltpu.VMEM((sz.rows + 8, LANES), jnp.int32),
            pltpu.VMEM((sz.stride, LANES), jnp.int32),
            pltpu.VMEM((count, LANES), jnp.float32),
        ],
        name=f"place_rows_{half}",
    )(words, words, gradient)


def state_call(sz, rows0, rows1, gradient):
    n = sz.tile_rows if sz.tile_rows % 16 == 0 else sz.rows
    tile = pl.BlockSpec((n, LANES), lambda i: (i, 0))
    return pl.pallas_call(
        state_kernel,
        grid=(sz.rows // n,),
        in_specs=[tile] * 3,
        out_specs=[tile] * 3,
        out_shape=[jax.ShapeDtypeStruct((sz.rows, LANES), jnp.float32)] * 3,
        name="state_rows",
    )(rows0, rows1, gradient)


def join_call(sz, first, other):
    total = sz.w_rows * sz.n_tensor
    n = next(k for k in (32, 16, 8, total) if total % k == 0)
    return pl.pallas_call(
        join_kernel,
        grid=(total // n,),
        in_specs=[pl.BlockSpec((n, FF_WIN // 2), lambda i: (i, 0))] * 2,
        out_specs=pl.BlockSpec((n, FF_WIN), lambda i: (i, 0)),
        out_shape=jax.ShapeDtypeStruct((total, FF_WIN), jnp.bfloat16),
        name="join_halves",
    )(first, other)


def per_device(master, moment, second, gradient, source_block):
    n_dp = lax.axis_size("dp")
    n_tensor = lax.axis_size("tensor")
    sz = Sizes(master.shape[0], n_dp * n_tensor, n_tensor)
    meta = index_call(sz, source_block)
    sent = pack_call(sz, meta, master, moment, second)
    halves, kept = [], []
    for half in range(2):
        words = lax.all_to_all(
            sent[half], ("dp", "tensor"), split_axis=0, concat_axis=0, tiled=True
        )
        rows, words = place_call(sz, half, words, gradient)
        kept.append(words)
        halves.append(lax.all_gather(rows, "tensor", axis=0, tiled=True))
    outs = state_call(sz, kept[0], kept[1], gradient)
    weight = join_call(sz, *halves)
    return (*outs, weight)


def solution(mesh):
    rows = P(("dp", "tensor"), None)
    return jax.shard_map(
        per_device,
        mesh=mesh,
        in_specs=(rows, rows, rows, rows, P(("dp", "tensor"))),
        out_specs=(rows, rows, rows, P("dp", None)),
        check_vma=False,
    )
```

time: 777 us -> 684 us (0.88)
  Pallas kernels: 0 us -> 477 us
  local copies, waits for them, and re-layouts: 295 us -> 0 us
  waiting for transfers between devices: 162 us -> 0.04 us
  blocking collectives: 249 us -> 193 us
  other arithmetic: 43.1 us -> 0 us
  starting transfers between devices: 11.1 us -> 0.08 us
    pallas_call x0 -> x6, Pallas kernels: none -> 477 us  [the longest x2 225 us: place_call(): pl.pallas_call(functools.partial(place_kernel, sz, half), grid=(sources +...]
    gather x12 -> x0, local copies, waits for them, and re-layouts: 258 us -> none  [the longest x6 83.7 us: per_device(): state[source_rows]]
    all_gather x1 -> x2, waiting for transfers between devices: 108 us -> 0.01 us  [per_device(): halves.append(lax.all_gather(rows, 'tensor', axis=0, tiled=True))]
    all_to_all x2, blocking collectives: 249 us -> 193 us  [per_device(): lax.all_to_all(sent[half], ('dp', 'tensor'), split_axis=0, concat_axis=0,...]
    all_to_all x2 -> x0, waiting for transfers between devices: 54.5 us -> none  [per_device(): lax.all_to_all(packed, ('dp', 'tensor'), split_axis=0, concat_axis=0, til...]
    reshape x4 -> x0, local copies, waits for them, and re-layouts: 18.7 us -> none  [the longest x3 16.1 us: per_device(): arranged = tuple((state.reshape(-1, 128)[placing] for state in arrived[:3]))]
    unnamed x3 -> x0, local copies, waits for them, and re-layouts: 17.4 us -> none
    sort x2 -> x0, other arithmetic: 16.5 us -> none  [the longest x1 8.24 us: per_device(): ordering = jnp.argsort(target, stable=True)]
  transfers between devices with their start and end apart: 3 -> 2, of which waited for: 2 -> 0; matrix products, arithmetic and copies ran while one was open for 21% -> 0% of each run, Pallas kernels for 0% -> 26%
where the time goes in v1:
time: 684 us
  Pallas kernels  477 us (70%)
  blocking collectives  193 us (28%)
  between operations  14 us (2%)
    pallas_call x2, Pallas kernels, place_call(): pl.pallas_call(functools.partial(place_kernel, sz, half), grid=(sources +...  225 us
    all_to_all x2, blocking collectives, per_device(): lax.all_to_all(sent[half], ('dp', 'tensor'), split_axis=0, concat_axis=0,...  193 us
    pallas_call x1, Pallas kernels, join_call(): pl.pallas_call(join_kernel, grid=(total // n,), in_specs=[pl.BlockSpec((n...  102 us
    pallas_call x1, Pallas kernels, pack_call(): pl.pallas_call(functools.partial(pack_kernel, sz), grid=(sz.tiles + sz.de...  76.2 us
    pallas_call x1, Pallas kernels, state_call(): pl.pallas_call(state_kernel, grid=(sz.rows // n,), in_specs=[tile] * 3, o...  68.6 us
  transfers between devices with their start and end apart: 2, of which 0 were waited for; matrix products, arithmetic and copies ran while one was open for 0% of the time, Pallas kernels for 26%

profile of v1, /device:TPU:0, one launch (start us, length us, event | category | flops | bytes accessed | tf_op | source)
XLA Modules:
  0.0 684.1 jit_solution(10117379828999601362)
XLA Ops:
  7.2 0.0 all-gather.5.cloned.1.call-start
  7.2 5.4 bucket_index.1.meta
  12.6 76.2 %pack_rows.1 = (s32[32,248,128]{2,1,0:T(8,128)}, s32[32,248,128]{2,1,0:T(8,128)}) custom-call(s32[81,128]{1,0:T(8,128)} %bucket_index.1.meta, f32[10368,128]{1,0:T(8,128)} %master.1, f32[10368,128]{1,0:T(8,128)} %moment.1, f32[10368,128]{1,0:T(8,128)} %second.1), custom_call_target="tpu_custom_call" | custom-call | tf_op jit(solution)/shard_map/pack_rows/pallas_call | solution.py:348
  88.8 98.2 %all_to_all.10.slots.words = s32[32,248,128]{2,1,0:T(8,128)} all-to-all(s32[32,248,128]{2,1,0:T(8,128)} %get-tuple-element.15), channel_id=1, replica_groups=mesh['dp'=4,'tensor'=8] {'dp','tensor'}, dimensions={0} | all-to-all | bytes 8126464 | tf_op jit(solution)/shard_map/all_to_all | solution.py:432
  187.0 112.5 %place_rows_1.1 = (bf16[72,9216]{1,0:T(8,128)(2,1)}, s32[10368,128]{1,0:T(8,128)}) custom-call(s32[32,248,128]{2,1,0:T(8,128)} %all_to_all.10.slots.words, s32[32,248,128]{2,1,0:T(8,128)} %all_to_all.10.slots.words, bf16[10368,128]{1,0:T(8,128)(2,1)} %grad.5), custom_call_target="tpu_custom_call" | custom-call | tf_op jit(solution)/shard_map/place_rows_1/pallas_call | solution.py:369
  299.5 0.0 all-gather.5.cloned.1.call-update
  299.5 0.0 all-gather.3.cloned.1.call-start
  299.6 94.6 %all_to_all.11.slots.words = s32[32,248,128]{2,1,0:T(8,128)} all-to-all(s32[32,248,128]{2,1,0:T(8,128)} %get-tuple-element.13), channel_id=1, replica_groups=mesh['dp'=4,'tensor'=8] {'dp','tensor'}, dimensions={0} | all-to-all | bytes 8126464 | tf_op jit(solution)/shard_map/all_to_all | solution.py:432
  394.2 112.5 %place_rows_0.1 = (bf16[72,9216]{1,0:T(8,128)(2,1)}, s32[10368,128]{1,0:T(8,128)}) custom-call(s32[32,248,128]{2,1,0:T(8,128)} %all_to_all.11.slots.words, s32[32,248,128]{2,1,0:T(8,128)} %all_to_all.11.slots.words, bf16[10368,128]{1,0:T(8,128)(2,1)} %grad.5), custom_call_target="tpu_custom_call" | custom-call | tf_op jit(solution)/shard_map/place_rows_0/pallas_call | solution.py:369
  506.6 0.0 all-gather.3.cloned.1.call-update
  506.7 68.6 %state_rows.1 = (f32[10368,128]{1,0:T(8,128)}, f32[10368,128]{1,0:T(8,128)}, f32[10368,128]{1,0:T(8,128)}) custom-call(s32[10368,128]{1,0:T(8,128)} %get-tuple-element.14.rows0, s32[10368,128]{1,0:T(8,128)} %get-tuple-element.16.rows1, bf16[10368,128]{1,0:T(8,128)(2,1)} %grad.5), custom_call_target="tpu_custom_call" | custom-call | tf_op jit(solution)/shard_map/state_rows/pallas_call | solution.py:401
  575.3 0.0 all-gather.5.cloned.1.call-done.other
  575.3 0.0 all-gather.3.cloned.1.call-done.first
  575.3 102.0 %join_halves.1 = bf16[576,18432]{1,0:T(8,128)(2,1)} custom-call(bf16[576,9216]{1,0:T(8,128)(2,1)} %all-gather.3.cloned.1.call-done.first, bf16[576,9216]{1,0:T(8,128)(2,1)} %all-gather.5.cloned.1.call-done.other), custom_call_target="tpu_custom_call" | custom-call | tf_op jit(solution)/shard_map/join_halves/pallas_call | solution.py:414
Async XLA Ops:
  7.2 568.1 %all-gather.5.cloned.1.call-start = ((), (), s32[]{:S(2)}) async-start(), calls=%async_computation.3 | async-start | bytes 11943936 | tf_op jit(solution)/shard_map/all_gather | solution.py:437
  299.5 275.7 %all-gather.3.cloned.1.call-start = ((), (), s32[]{:S(2)}) async-start(), calls=%async_computation.2 | async-start | bytes 11943936 | tf_op jit(solution)/shard_map/all_gather | solution.py:437
Sparse Core Ops, SparseCore 0:
  299.7 101.5 all-gather.4
  506.8 63.0 all-gather.2

commit v2 on v1

--- a/solution.py
+++ b/solution.py
@@ -58,6 +58,10 @@
     )
     master_new = master - learn_rate * (ratio + weight_decay * master)
     return (master_new, moment_new, second_new)
+
+
+def cost(micros, moved):
+    return pl.CostEstimate(flops=int(micros * 1e9), bytes_accessed=moved, transcendentals=0)
 
 
 def round_up(value, step):
@@ -124,18 +128,19 @@
     return lax.broadcasted_iota(jnp.int32, shape, 1)
 
 
-def pack_kernel(sz, meta, master, moment, second, out0, out1, rows_w, rows_s, code_w, code_s):
+def pack_kernel(sz, meta, master, moment, second, out0, out1, rows, code_w, code_s):
     step = pl.program_id(0)
+    rows_w, rows_s = rows.at[0], rows.at[1]
 
     @pl.when(step == 0)
     def _():
-        def fill(i, carry):
-            rows_s[pl.ds(pl.multiple_of(i * 8, 8), 8), :] = jnp.full(
-                (8, LANES), sz.rows << 16, jnp.int32
+        def fill(d, carry):
+            rows_s[pl.ds(pl.multiple_of(d * sz.stride, 8), sz.stride), :] = jnp.full(
+                (sz.stride, LANES), sz.rows << 16, jnp.int32
             )
             return carry
 
-        lax.fori_loop(0, sz.stride * sz.devices // 8, fill, 0)
+        lax.fori_loop(0, sz.devices, fill, 0)
 
     @pl.when(step < sz.tiles)
     def _():
@@ -144,19 +149,23 @@
         code_w[...] = (code_m << 16) | (code_v & 0xFFFF)
         code_s[...] = second_code(second[...])
 
+        lines = sz.tile_rows // sz.seg
+
         def body(i, carry):
-            first = step * sz.tile_rows + i * 8
-            line, at = first // sz.seg, first % sz.seg
-            words = [code_w[pl.ds(i * 8 + u, 1), :] for u in range(8)]
-            seconds = [code_s[pl.ds(i * 8 + u, 1), :] for u in range(8)]
-            for u in range(8):
-                m = meta[line, at + u]
-                to = m & 0xFFFF
-                rows_w[pl.ds(to, 1), :] = words[u]
-                rows_s[pl.ds(to, 1), :] = seconds[u] | ((m >> 16) << 16)
+            line = step * lines + i
+            for at in range(0, sz.seg, 8):
+                first = pl.multiple_of(i * sz.seg, 8) + at
+                words = [code_w[pl.ds(first + u, 1), :] for u in range(8)]
+                seconds = [code_s[pl.ds(first + u, 1), :] for u in range(8)]
+                for u in range(8):
+                    m = meta[line, at + u]
+                    to = m & 0xFFFF
+                    slot = jnp.broadcast_to(m, (1, LANES)) & -65536
+                    rows_w[pl.ds(to, 1), :] = words[u]
+                    rows_s[pl.ds(to, 1), :] = seconds[u] | slot
             return carry
 
-        lax.fori_loop(0, sz.tile_rows // 8, body, 0)
+        lax.fori_loop(0, lines, body, 0)
 
     @pl.when(step >= sz.tiles)
     def _():
@@ -254,17 +263,12 @@
                 x = [words[s, at + p * sz.tail : at + (p + 1) * sz.tail, :] for p in range(3)]
                 group(sz.main, sz.tail, *x)
 
-            unroll = next(n for n in (3, 2, 1) if sz.groups % n == 0) * 4
-
-            def body(i, carry):
-                values = [line[pl.ds(i * unroll + u, 1), :] for u in range(unroll)]
-                for u in range(unroll):
-                    j = i * unroll + u
-                    to = slots[s, sz.slot_at % 8 + j // LANES, j % LANES]
+            for j in range(0, 4 * sz.groups, 4):
+                values = [line[j + u : j + u + 1, :] for u in range(4)]
+                for u in range(4):
+                    r, c = divmod(j + u, LANES)
+                    to = slots[s, sz.slot_at % 8 + r, c]
                     rows[pl.ds(to, 1), :] = values[u]
-                return carry
-
-            lax.fori_loop(0, 4 * sz.groups // unroll, body, 0)
             return carry
 
         lax.fori_loop(0, sz.dests, one, 0)
@@ -276,24 +280,29 @@
         kept[...] = rows[pl.ds(base, count), :]
         grad_f32[...] = grad[...].astype(jnp.float32)
         low = lane_of((sz.w_tile, LANES)) < HALF
-        unroll = next(n for n in (4, 3, 2, 1) if (sz.w_blocks // 2) % n == 0)
+        unroll = next(n for n in (8, 6, 4, 3, 2, 1) if (sz.w_blocks // 2) % n == 0)
 
         def body(i, carry):
+            loaded = []
             for u in range(unroll):
                 c = i * unroll + u
-                even = rows[pl.ds(base + 2 * c, sz.w_tile, stride=sz.w_blocks), :]
-                odd = rows[pl.ds(base + 2 * c + 1, sz.w_tile, stride=sz.w_blocks), :]
-                g_even = grad_f32[pl.ds(2 * c, sz.w_tile, stride=sz.w_blocks), :]
-                g_odd = grad_f32[pl.ds(2 * c + 1, sz.w_tile, stride=sz.w_blocks), :]
+                loaded.append(
+                    tuple(
+                        ref[pl.ds(first + 2 * c + odd, sz.w_tile, stride=sz.w_blocks), :]
+                        for ref, first in ((rows, base), (grad_f32, 0))
+                        for odd in range(2)
+                    )
+                )
+            for u in range(unroll):
+                even, odd, g_even, g_odd = loaded[u]
                 if half == 0:
                     g_odd = pltpu.roll(g_odd, HALF, 1)
                 else:
                     g_even = pltpu.roll(g_even, HALF, 1)
                 master, moment, second = decode_pair(even, odd)
                 new, _, _ = adam_step(master, moment, second, jnp.where(low, g_even, g_odd))
-                weight[:, pl.ds(pl.multiple_of(c * LANES, LANES), LANES)] = new.astype(
-                    jnp.bfloat16
-                )
+                at = pl.multiple_of((i * unroll + u) * LANES, LANES)
+                weight[:, pl.ds(at, LANES)] = new.astype(jnp.bfloat16)
             return carry
 
         lax.fori_loop(0, sz.w_blocks // 2 // unroll, body, 0)
@@ -301,33 +310,36 @@
 
 def state_kernel(rows0, rows1, grad, master_out, moment_out, second_out):
     n = rows0.shape[0]
+    some = next(k for k in (64, 48, 32, 16) if n % k == 0)
 
     def body(i, carry):
-        at = pl.ds(pl.multiple_of(i * 16, 16), 16)
+        at = pl.ds(pl.multiple_of(i * some, some), some)
         master, moment, second = decode_pair(rows0[at, :], rows1[at, :])
         new = adam_step(master, moment, second, grad[at, :].astype(jnp.float32))
         master_out[at, :], moment_out[at, :], second_out[at, :] = new
         return carry
 
-    lax.fori_loop(0, n // 16, body, 0)
+    lax.fori_loop(0, n // some, body, 0)
 
 
 def join_kernel(first, other, weight):
     blocks = first.shape[1] // LANES
+    unroll = next(n for n in (6, 4, 3, 2, 1) if blocks % n == 0)
     low = lane_of((first.shape[0], LANES)) < HALF
 
-    def body(c, carry):
-        at = pl.ds(pl.multiple_of(c * LANES, LANES), LANES)
-        a = first[:, at].astype(jnp.float32)
-        b = other[:, at].astype(jnp.float32)
-        even = jnp.where(low, a, pltpu.roll(b, HALF, 1))
-        odd = jnp.where(low, pltpu.roll(a, HALF, 1), b)
-        to = pl.multiple_of(c * 2 * LANES, 2 * LANES)
-        weight[:, pl.ds(to, LANES)] = even.astype(jnp.bfloat16)
-        weight[:, pl.ds(pl.multiple_of(to + LANES, LANES), LANES)] = odd.astype(jnp.bfloat16)
+    def body(i, carry):
+        at = [pl.multiple_of((i * unroll + u) * LANES, LANES) for u in range(unroll)]
+        a = [first[:, pl.ds(x, LANES)].astype(jnp.float32) for x in at]
+        b = [other[:, pl.ds(x, LANES)].astype(jnp.float32) for x in at]
+        for u in range(unroll):
+            even = jnp.where(low, a[u], pltpu.roll(b[u], HALF, 1))
+            odd = jnp.where(low, pltpu.roll(a[u], HALF, 1), b[u])
+            to = pl.multiple_of(at[u] * 2, 2 * LANES)
+            weight[:, pl.ds(to, LANES)] = even.astype(jnp.bfloat16)
+            weight[:, pl.ds(pl.multiple_of(to + LANES, LANES), LANES)] = odd.astype(jnp.bfloat16)
         return carry
 
-    lax.fori_loop(0, blocks, body, 0)
+    lax.fori_loop(0, blocks // unroll, body, 0)
 
 
 def index_call(sz, source_block):
@@ -352,8 +364,7 @@
         out_specs=[piece, piece],
         out_shape=[jax.ShapeDtypeStruct((sz.devices, sz.piece, LANES), jnp.int32)] * 2,
         scratch_shapes=[
-            pltpu.VMEM((total, LANES), jnp.int32),
-            pltpu.VMEM((total, LANES), jnp.int32),
+            pltpu.VMEM((2, total, LANES), jnp.int32),
             pltpu.VMEM((sz.tile_rows, LANES), jnp.int32),
             pltpu.VMEM((sz.tile_rows, LANES), jnp.int32),
         ],
@@ -391,6 +402,7 @@
             pltpu.VMEM((sz.stride, LANES), jnp.int32),
             pltpu.VMEM((count, LANES), jnp.float32),
         ],
+        cost_estimate=cost(25, 16 * LANES * sz.rows),
         name=f"place_rows_{half}",
     )(words, words, gradient)
 
@@ -404,6 +416,7 @@
         in_specs=[tile] * 3,
         out_specs=[tile] * 3,
         out_shape=[jax.ShapeDtypeStruct((sz.rows, LANES), jnp.float32)] * 3,
+        cost_estimate=cost(15, 22 * LANES * sz.rows),
         name="state_rows",
     )(rows0, rows1, gradient)
 

time: 684 us -> 398 us (0.58)
  Pallas kernels: 477 us -> 155 us
  waiting for transfers between devices: 0.04 us -> 35.1 us
    pallas_call x2, Pallas kernels: 225 us -> 59.1 us  [place_call(): pl.pallas_call(functools.partial(place_kernel, sz, half), grid=(sources +...]
    pallas_call x1, Pallas kernels: 102 us -> 28.2 us  [join_call(): pl.pallas_call(join_kernel, grid=(total // n,), in_specs=[pl.BlockSpec((n...]
    pallas_call x1, Pallas kernels: 76.2 us -> 34.7 us  [pack_call(): pl.pallas_call(functools.partial(pack_kernel, sz), grid=(sz.tiles + sz.de...]
    pallas_call x1, Pallas kernels: 68.6 us -> 27.8 us  [state_call(): pl.pallas_call(state_kernel, grid=(sz.rows // n,), in_specs=[tile] * 3, o...]
    all_gather x2, waiting for transfers between devices: 0.01 us -> 35.1 us  [per_device(): halves.append(lax.all_gather(rows, 'tensor', axis=0, tiled=True))]
  transfers between devices with their start and end apart: 2 -> 2, of which waited for: 0 -> 1; matrix products, arithmetic and copies ran while one was open for 0% -> 0% of each run, Pallas kernels for 26% -> 14%
where the time goes in v2:
time: 398 us; the launch traced here: 397 us
  blocking collectives  193 us (48%)
  Pallas kernels  155 us (39%)
  waiting for transfers between devices  35.1 us (9%)
  between operations  14 us (4%)
    all_to_all x2, blocking collectives, per_device(): lax.all_to_all(sent[half], ('dp', 'tensor'), split_axis=0, concat_axis=0,...  193 us
    pallas_call x2, Pallas kernels, place_call(): pl.pallas_call(functools.partial(place_kernel, sz, half), grid=(sources +...  59.1 us
    all_gather x2, waiting for transfers between devices, per_device(): halves.append(lax.all_gather(rows, 'tensor', axis=0, tiled=True))  35.1 us
    pallas_call x1, Pallas kernels, pack_call(): pl.pallas_call(functools.partial(pack_kernel, sz), grid=(sz.tiles + sz.de...  34.7 us
    pallas_call x1, Pallas kernels, join_call(): pl.pallas_call(join_kernel, grid=(total // n,), in_specs=[pl.BlockSpec((n...  28.2 us
    pallas_call x1, Pallas kernels, state_call(): pl.pallas_call(state_kernel, grid=(sz.rows // n,), in_specs=[tile] * 3, o...  27.8 us
  transfers between devices with their start and end apart: 2, of which 1 were waited for; matrix products, arithmetic and copies ran while one was open for 0% of the time, Pallas kernels for 14%

profile of v2, /device:TPU:0, one launch (start us, length us, event | category | flops | bytes accessed | tf_op | source)
XLA Modules:
  0.0 397.3 jit_solution(14533513882649616204)
XLA Ops:
  7.2 0.0 all-gather.5.cloned.1.call-start
  7.2 5.4 %bucket_index.1.meta = s32[81,128]{1,0:T(8,128)} custom-call(s32[81,128]{1,0:T(8,128)} %bitcast.1), custom_call_target="tpu_custom_call" | custom-call | tf_op jit(solution)/shard_map/bucket_index/pallas_call | solution.py:347
  12.6 34.7 %pack_rows.1 = (s32[32,248,128]{2,1,0:T(8,128)}, s32[32,248,128]{2,1,0:T(8,128)}) custom-call(s32[81,128]{1,0:T(8,128)} %bucket_index.1.meta, f32[10368,128]{1,0:T(8,128)} %master.1, f32[10368,128]{1,0:T(8,128)} %moment.1, f32[10368,128]{1,0:T(8,128)} %second.1), custom_call_target="tpu_custom_call" | custom-call | tf_op jit(solution)/shard_map/pack_rows/pallas_call | solution.py:360
  47.3 98.2 %all_to_all.10.slots.words = s32[32,248,128]{2,1,0:T(8,128)} all-to-all(s32[32,248,128]{2,1,0:T(8,128)} %get-tuple-element.15), channel_id=1, replica_groups=mesh['dp'=4,'tensor'=8] {'dp','tensor'}, dimensions={0} | all-to-all | bytes 8126464 | tf_op jit(solution)/shard_map/all_to_all | solution.py:445
  145.6 29.5 %place_rows_1.1 = (bf16[72,9216]{1,0:T(8,128)(2,1)}, s32[10368,128]{1,0:T(8,128)}) custom-call(s32[32,248,128]{2,1,0:T(8,128)} %all_to_all.10.slots.words, s32[32,248,128]{2,1,0:T(8,128)} %all_to_all.10.slots.words, bf16[10368,128]{1,0:T(8,128)(2,1)} %grad.5), custom_call_target="tpu_custom_call" | custom-call | flops 24999999488 | bytes 21233664 | tf_op jit(solution)/shard_map/place_rows_1/pallas_call | solution.py:380
  175.1 0.0 all-gather.5.cloned.1.call-update
  175.1 0.0 all-gather.3.cloned.1.call-start
  175.2 94.6 %all_to_all.11.slots.words = s32[32,248,128]{2,1,0:T(8,128)} all-to-all(s32[32,248,128]{2,1,0:T(8,128)} %get-tuple-element.13), channel_id=1, replica_groups=mesh['dp'=4,'tensor'=8] {'dp','tensor'}, dimensions={0} | all-to-all | bytes 8126464 | tf_op jit(solution)/shard_map/all_to_all | solution.py:445
  269.8 29.5 %place_rows_0.1 = (bf16[72,9216]{1,0:T(8,128)(2,1)}, s32[10368,128]{1,0:T(8,128)}) custom-call(s32[32,248,128]{2,1,0:T(8,128)} %all_to_all.11.slots.words, s32[32,248,128]{2,1,0:T(8,128)} %all_to_all.11.slots.words, bf16[10368,128]{1,0:T(8,128)(2,1)} %grad.5), custom_call_target="tpu_custom_call" | custom-call | flops 24999999488 | bytes 21233664 | tf_op jit(solution)/shard_map/place_rows_0/pallas_call | solution.py:380
  299.3 0.0 all-gather.3.cloned.1.call-update
  299.3 27.8 %state_rows.1 = (f32[10368,128]{1,0:T(8,128)}, f32[10368,128]{1,0:T(8,128)}, f32[10368,128]{1,0:T(8,128)}) custom-call(s32[10368,128]{1,0:T(8,128)} %get-tuple-element.14.rows0, s32[10368,128]{1,0:T(8,128)} %get-tuple-element.16.rows1, bf16[10368,128]{1,0:T(8,128)(2,1)} %grad.5), custom_call_target="tpu_custom_call" | custom-call | flops 15000000512 | bytes 29196288 | tf_op jit(solution)/shard_map/state_rows/pallas_call | solution.py:413
  327.2 0.0 all-gather.5.cloned.1.call-done.other
  327.2 35.1 %all-gather.3.cloned.1.call-done.first = bf16[576,9216]{1,0:T(8,128)(2,1)} async-done(((bf16[72,9216]{1,0:T(8,128)(2,1)}), bf16[576,9216]{1,0:T(8,128)(2,1)}) %all-gather.3.cloned.1.call-update) | async-done | bytes 10616848 | tf_op jit(solution)/shard_map/all_gather | solution.py:450
  362.3 28.2 %join_halves.1 = bf16[576,18432]{1,0:T(8,128)(2,1)} custom-call(bf16[576,9216]{1,0:T(8,128)(2,1)} %all-gather.3.cloned.1.call-done.first, bf16[576,9216]{1,0:T(8,128)(2,1)} %all-gather.5.cloned.1.call-done.other), custom_call_target="tpu_custom_call" | custom-call | tf_op jit(solution)/shard_map/join_halves/pallas_call | solution.py:427
Async XLA Ops:
  7.2 320.0 %all-gather.5.cloned.1.call-start = ((), (), s32[]{:S(2)}) async-start(), calls=%async_computation.3 | async-start | bytes 11943936 | tf_op jit(solution)/shard_map/all_gather | solution.py:450
  175.1 187.1 %all-gather.3.cloned.1.call-start = ((), (), s32[]{:S(2)}) async-start(), calls=%async_computation.2 | async-start | bytes 11943936 | tf_op jit(solution)/shard_map/all_gather | solution.py:450
Sparse Core Ops, SparseCore 0:
  175.3 101.5 all-gather.4
  299.4 62.7 all-gather.2

commit v3 on v2

--- a/solution.py
+++ b/solution.py
@@ -7,6 +7,7 @@
 from jax.experimental import pallas as pl
 from jax.experimental.pallas import tpu as pltpu
 from jax.sharding import PartitionSpec as P
+
 
 FF_WIN = 18432
 LANES = 128
@@ -42,7 +43,7 @@
 
 
 def second_code(x):
-    return jnp.minimum(jnp.sqrt(x) * SECOND_STEPS + 0.5, 65535.0).astype(jnp.int32)
+    return jnp.minimum(x * lax.rsqrt(x) * SECOND_STEPS + 0.5, 65535.0).astype(jnp.int32)
 
 
 def second_value(code):
@@ -53,9 +54,8 @@
 def adam_step(master, moment, second, grad_vals):
     moment_new = decay_one * moment + (1.0 - decay_one) * grad_vals
     second_new = decay_two * second + (1.0 - decay_two) * grad_vals * grad_vals
-    ratio = (moment_new * (1.0 / correct_one)) / (
-        jnp.sqrt(second_new * (1.0 / correct_two)) + epsilon
-    )
+    level = second_new * (1.0 / correct_two)
+    ratio = (moment_new * (1.0 / correct_one)) / (level * lax.rsqrt(level) + epsilon)
     master_new = master - learn_rate * (ratio + weight_decay * master)
     return (master_new, moment_new, second_new)
 
@@ -86,20 +86,26 @@
         self.piece = round_up(words + self.slot_rows, 8)
         self.slot_tile = self.slot_at // 8
         self.seg = math.gcd(rows, LANES)
-        self.tiles = next(n for n in (9, 8, 6, 4, 3, 2, 1) if rows % (8 * n) == 0)
+        self.lines = rows // self.seg
+        self.tiles = next(n for n in (3, 2, 4, 1) if self.lines % n == 0)
         self.tile_rows = rows // self.tiles
-        self.dests = next(n for n in (4, 2, 1) if devices % n == 0)
+        self.tile_lines = self.lines // self.tiles
+        self.dests = next(n for n in (8, 4, 2, 1) if devices % n == 0)
+        self.sources = next(n for n in (8, 4, 2, 1) if devices % n == 0)
         self.w_rows = rows * LANES // FF_WIN
         self.w_blocks = FF_WIN // LANES
-        self.w_tile = 8 if self.w_rows % 8 == 0 else self.w_rows
+        self.w_tile = next((n for n in (24, 16, 8) if self.w_rows % n == 0), self.w_rows)
         self.w_tiles = self.w_rows // self.w_tile
         assert self.stride * devices < 65536 and rows < 32768 and self.seg % 8 == 0
         assert self.piece - 8 * self.slot_tile == 8 and self.w_blocks % 2 == 0
 
 
-def index_kernel(sz, block_ref, meta_ref):
-    n, seg = block_ref.shape
-    block = block_ref[...]
+def lane_of(shape):
+    return lax.broadcasted_iota(jnp.int32, shape, 1)
+
+
+def bucket_index(sz, block):
+    n, seg = block.shape
     target = ((block.astype(jnp.float32) + 0.5) * (1.0 / sz.rows)).astype(jnp.int32)
     slot = block - target * sz.rows
     at = lax.broadcasted_iota(jnp.int32, (seg, 2 * seg), 0)
@@ -121,102 +127,156 @@
         return rank
 
     rank = lax.fori_loop(0, (sz.devices + 7) // 8, body, jnp.zeros((n, seg), jnp.float32))
-    meta_ref[...] = (slot << 16) | (target * sz.stride + rank.astype(jnp.int32))
-
-
-def lane_of(shape):
-    return lax.broadcasted_iota(jnp.int32, shape, 1)
-
-
-def pack_kernel(sz, meta, master, moment, second, out0, out1, rows, code_w, code_s):
+    return (slot << 16) | (target * sz.stride + rank.astype(jnp.int32))
+
+
+def fill_rows(sz, rows):
+    def fill(d, carry):
+        at = pl.ds(pl.multiple_of(d * sz.stride, 8), sz.stride)
+        rows[at, :] = jnp.full((sz.stride, LANES), sz.rows << 16, jnp.int32)
+        return carry
+
+    lax.fori_loop(0, sz.devices, fill, 0)
+
+
+def encode_lines(sz, states, i, first_half, other_half):
+    at = pl.ds(pl.multiple_of(i * sz.seg, 8), sz.seg)
+    master, moment, second = (state[at, :] for state in states)
+    code_m = log_code(master, MASTER_INV, MASTER_STEPS)
+    code_v = log_code(moment, MOMENT_INV, MOMENT_STEPS)
+    word = (code_m << 16) | (code_v & 0xFFFF)
+    code_s = second_code(second)
+    pair = code_s | (pltpu.roll(code_s, LANES - QUARTER, 1) << 16)
+    lane = lane_of(word.shape)
+    used = lane < HALF + QUARTER
+    first_half[...] = jnp.where(
+        lane < HALF, word, jnp.where(used, pltpu.roll(pair, HALF, 1), 0)
+    )
+    other_half[at, :] = jnp.where(
+        lane < HALF, pltpu.roll(word, HALF, 1), jnp.where(used, pair, 0)
+    )
+
+
+def scatter_line(sz, meta, line, words, base, rows):
+    free = lane_of((1, LANES)) >= HALF + QUARTER
+    for at in range(0, sz.seg, 8):
+        values = [words[pl.ds(base + at + u, 1), :] for u in range(8)]
+        for u in range(8):
+            m = meta[line, at + u]
+            rows[pl.ds(m & 0xFFFF, 1), :] = jnp.where(free, m, values[u])
+
+
+def pack_piece(sz, rows, base, out, dd):
+    def group(at, n):
+        lane = lane_of((n, LANES))
+        low = lane < HALF
+        r = [rows[pl.ds(base + 4 * at + q, n, stride=4), :] for q in range(4)]
+        seconds = jnp.where(
+            low,
+            jnp.where(
+                lane < QUARTER, pltpu.roll(r[0], HALF, 1), pltpu.roll(r[1], LANES - QUARTER, 1)
+            ),
+            jnp.where(lane < HALF + QUARTER, r[2], pltpu.roll(r[3], QUARTER, 1)),
+        )
+        return (
+            jnp.where(low, r[0], pltpu.roll(r[1], HALF, 1)),
+            jnp.where(low, r[2], pltpu.roll(r[3], HALF, 1)),
+            seconds,
+        )
+
+    for t in range(sz.main // 8):
+        for p, x in enumerate(group(8 * t, 8)):
+            out[dd, p * sz.main + 8 * t : p * sz.main + 8 * t + 8, :] = x
+    if sz.tail:
+        for p, x in enumerate(group(sz.main, sz.tail)):
+            at = 3 * sz.main + p * sz.tail
+            out[dd, at : at + sz.tail, :] = x
+    for g in range(sz.slot_rows):
+        line = jnp.zeros((1, LANES), jnp.int32)
+        for k in range(LANES // QUARTER):
+            first = g * LANES + k * QUARTER
+            n = min(QUARTER, sz.stride - first)
+            if n <= 0:
+                continue
+            slots = rows[pl.ds(base + first, n), :] >> 16
+            row = lax.broadcasted_iota(jnp.int32, (n, LANES), 0) + HALF + QUARTER
+            some = jnp.sum(
+                jnp.where(row == lane_of((n, LANES)), slots, 0), axis=0, keepdims=True
+            )
+            shift = (QUARTER * (k + 1)) % LANES
+            line = line + (pltpu.roll(some, shift, 1) if shift else some)
+        out[dd, sz.slot_at + g : sz.slot_at + g + 1, :] = line
+
+
+def pack_dests(sz, step, rows, out):
+    def one(dd, carry):
+        base = pl.multiple_of((step * sz.dests + dd) * sz.stride, 8)
+        pack_piece(sz, rows, base, out, dd)
+        return carry
+
+    lax.fori_loop(0, sz.dests, one, 0)
+
+
+def pack_first_kernel(
+    sz, block, master, moment, second, out, other, meta_out, rows, meta, meta_vec, even, odd, sem
+):
     step = pl.program_id(0)
-    rows_w, rows_s = rows.at[0], rows.at[1]
 
     @pl.when(step == 0)
     def _():
-        def fill(d, carry):
-            rows_s[pl.ds(pl.multiple_of(d * sz.stride, 8), sz.stride), :] = jnp.full(
-                (sz.stride, LANES), sz.rows << 16, jnp.int32
-            )
+        meta_vec[...] = bucket_index(sz, block[...])
+        copies = [
+            pltpu.make_async_copy(meta_vec, meta, sem.at[0]),
+            pltpu.make_async_copy(meta_vec, meta_out, sem.at[1]),
+        ]
+        for copy in copies:
+            copy.start()
+        fill_rows(sz, rows)
+        for copy in copies:
+            copy.wait()
+
+    @pl.when(step < sz.tiles)
+    def _():
+        states = (master, moment, second)
+        n = sz.tile_lines
+        encode_lines(sz, states, 0, even, other)
+
+        def body(i, carry):
+            line = step * n + 2 * i
+            scatter_line(sz, meta, line, even, 0, rows)
+            encode_lines(sz, states, 2 * i + 1, odd, other)
+            scatter_line(sz, meta, line + 1, odd, 0, rows)
+            encode_lines(sz, states, jnp.minimum(2 * i + 2, n - 1), even, other)
             return carry
 
-        lax.fori_loop(0, sz.devices, fill, 0)
+        lax.fori_loop(0, n // 2, body, 0)
+        if n % 2:
+            scatter_line(sz, meta, step * n + n - 1, even, 0, rows)
+
+    @pl.when(step >= sz.tiles)
+    def _():
+        pack_dests(sz, step - sz.tiles, rows, out)
+
+
+def pack_other_kernel(sz, meta, words, out, rows):
+    step = pl.program_id(0)
+
+    @pl.when(step == 0)
+    def _():
+        fill_rows(sz, rows)
 
     @pl.when(step < sz.tiles)
     def _():
-        code_m = log_code(master[...], MASTER_INV, MASTER_STEPS)
-        code_v = log_code(moment[...], MOMENT_INV, MOMENT_STEPS)
-        code_w[...] = (code_m << 16) | (code_v & 0xFFFF)
-        code_s[...] = second_code(second[...])
-
-        lines = sz.tile_rows // sz.seg
-
         def body(i, carry):
-            line = step * lines + i
-            for at in range(0, sz.seg, 8):
-                first = pl.multiple_of(i * sz.seg, 8) + at
-                words = [code_w[pl.ds(first + u, 1), :] for u in range(8)]
-                seconds = [code_s[pl.ds(first + u, 1), :] for u in range(8)]
-                for u in range(8):
-                    m = meta[line, at + u]
-                    to = m & 0xFFFF
-                    slot = jnp.broadcast_to(m, (1, LANES)) & -65536
-                    rows_w[pl.ds(to, 1), :] = words[u]
-                    rows_s[pl.ds(to, 1), :] = seconds[u] | slot
+            base = pl.multiple_of(i * sz.seg, 8)
+            scatter_line(sz, meta, step * sz.tile_lines + i, words, base, rows)
             return carry
 
-        lax.fori_loop(0, lines, body, 0)
+        lax.fori_loop(0, sz.tile_lines, body, 0)
 
     @pl.when(step >= sz.tiles)
     def _():
-        def one(dd, carry):
-            base = pl.multiple_of(((step - sz.tiles) * sz.dests + dd) * sz.stride, 8)
-
-            def group(at, n):
-                lane = lane_of((n, LANES))
-                low = lane < HALF
-                w = [rows_w[pl.ds(base + 4 * at + q, n, stride=4), :] for q in range(4)]
-                pairs = []
-                for q in range(4):
-                    s = rows_s[pl.ds(base + 4 * at + q, n, stride=4), :] & 0xFFFF
-                    pairs.append(s | (pltpu.roll(s, LANES - QUARTER, 1) << 16))
-                r = [pltpu.roll(x, HALF, 1) for x in w]
-                first = (jnp.where(low, w[0], r[1]), jnp.where(low, w[2], r[3]))
-                other = (jnp.where(low, r[0], w[1]), jnp.where(low, r[2], w[3]))
-                both = []
-                for h in range(2):
-                    joined = None
-                    for q in range(4):
-                        shift = (QUARTER * q - HALF * h) % LANES
-                        x = pltpu.roll(pairs[q], shift, 1) if shift else pairs[q]
-                        joined = x if q == 0 else jnp.where(lane < QUARTER * q, joined, x)
-                    both.append(joined)
-                return (first + (both[0],), other + (both[1],))
-
-            for t in range(sz.main // 8):
-                a, b = group(8 * t, 8)
-                for p in range(3):
-                    out0[dd, p * sz.main + 8 * t : p * sz.main + 8 * t + 8, :] = a[p]
-                    out1[dd, p * sz.main + 8 * t : p * sz.main + 8 * t + 8, :] = b[p]
-            if sz.tail:
-                a, b = group(sz.main, sz.tail)
-                for p in range(3):
-                    at = 3 * sz.main + p * sz.tail
-                    out0[dd, at : at + sz.tail, :] = a[p]
-                    out1[dd, at : at + sz.tail, :] = b[p]
-            for g in range(sz.slot_rows):
-                n = min(LANES, sz.stride - g * LANES)
-                slots = rows_s[pl.ds(base + g * LANES, n), :] >> 16
-                row = lax.broadcasted_iota(jnp.int32, (n, LANES), 0)
-                line = jnp.sum(
-                    jnp.where(row == lane_of((n, LANES)), slots, 0), axis=0, keepdims=True
-                )
-                at = sz.slot_at + g
-                out0[dd, at : at + 1, :] = line
-                out1[dd, at : at + 1, :] = line
-            return carry
-
-        lax.fori_loop(0, sz.dests, one, 0)
+        pack_dests(sz, step - sz.tiles, rows, out)
 
 
 def decode_pair(even, odd):
@@ -235,13 +295,13 @@
     return master, moment, second
 
 
-def place_kernel(sz, half, slots, words, grad, weight, kept, rows, line, grad_f32):
+def place_kernel(sz, half, slots, words, grad, weight, kept, rows, line, line_b, grad_f32):
     step = pl.program_id(0)
-    sources = sz.devices // sz.dests
+    sources = sz.devices // sz.sources
 
     @pl.when(step < sources)
     def _():
-        def one(s, carry):
+        def one(s, line):
             def group(at, n, x0, x1, x2):
                 low = lane_of((n, LANES)) < HALF
                 parts = (
@@ -263,15 +323,20 @@
                 x = [words[s, at + p * sz.tail : at + (p + 1) * sz.tail, :] for p in range(3)]
                 group(sz.main, sz.tail, *x)
 
+        def put(s, line):
             for j in range(0, 4 * sz.groups, 4):
                 values = [line[j + u : j + u + 1, :] for u in range(4)]
                 for u in range(4):
                     r, c = divmod(j + u, LANES)
                     to = slots[s, sz.slot_at % 8 + r, c]
                     rows[pl.ds(to, 1), :] = values[u]
-            return carry
-
-        lax.fori_loop(0, sz.dests, one, 0)
+
+        buffers = (line, line_b)
+        one(0, line)
+        for s in range(sz.sources):
+            if s + 1 < sz.sources:
+                one(s + 1, buffers[(s + 1) % 2])
+            put(s, buffers[s % 2])
 
     @pl.when(step >= sources)
     def _():
@@ -280,7 +345,7 @@
         kept[...] = rows[pl.ds(base, count), :]
         grad_f32[...] = grad[...].astype(jnp.float32)
         low = lane_of((sz.w_tile, LANES)) < HALF
-        unroll = next(n for n in (8, 6, 4, 3, 2, 1) if (sz.w_blocks // 2) % n == 0)
+        unroll = next(n for n in (4, 3, 2, 1) if (sz.w_blocks // 2) % n == 0)
 
         def body(i, carry):
             loaded = []
@@ -324,56 +389,67 @@
 
 def join_kernel(first, other, weight):
     blocks = first.shape[1] // LANES
-    unroll = next(n for n in (6, 4, 3, 2, 1) if blocks % n == 0)
+    unroll = next(n for n in (8, 6, 4, 3, 2, 1) if blocks % n == 0)
     low = lane_of((first.shape[0], LANES)) < HALF
 
     def body(i, carry):
         at = [pl.multiple_of((i * unroll + u) * LANES, LANES) for u in range(unroll)]
-        a = [first[:, pl.ds(x, LANES)].astype(jnp.float32) for x in at]
-        b = [other[:, pl.ds(x, LANES)].astype(jnp.float32) for x in at]
+        a = [first[:, pl.ds(x, LANES)] for x in at]
+        b = [other[:, pl.ds(x, LANES)] for x in at]
         for u in range(unroll):
-            even = jnp.where(low, a[u], pltpu.roll(b[u], HALF, 1))
-            odd = jnp.where(low, pltpu.roll(a[u], HALF, 1), b[u])
             to = pl.multiple_of(at[u] * 2, 2 * LANES)
-            weight[:, pl.ds(to, LANES)] = even.astype(jnp.bfloat16)
-            weight[:, pl.ds(pl.multiple_of(to + LANES, LANES), LANES)] = odd.astype(jnp.bfloat16)
+            next_to = pl.multiple_of(to + LANES, LANES)
+            weight[:, pl.ds(to, LANES)] = jnp.where(low, a[u], pltpu.roll(b[u], HALF, 1))
+            weight[:, pl.ds(next_to, LANES)] = jnp.where(low, pltpu.roll(a[u], HALF, 1), b[u])
         return carry
 
     lax.fori_loop(0, blocks // unroll, body, 0)
 
 
-def index_call(sz, source_block):
-    shape = (sz.rows // sz.seg, sz.seg)
-    return pl.pallas_call(
-        functools.partial(index_kernel, sz),
-        out_shape=jax.ShapeDtypeStruct(shape, jnp.int32),
-        name="bucket_index",
-    )(source_block.reshape(shape))
-
-
-def pack_call(sz, meta, master, moment, second):
+def pack_calls(sz, source_block, master, moment, second):
+    lines = (sz.lines, sz.seg)
     tile = pl.BlockSpec((sz.tile_rows, LANES), lambda i: (jnp.minimum(i, sz.tiles - 1), 0))
     piece = pl.BlockSpec(
         (sz.dests, sz.piece, LANES), lambda i: (jnp.maximum(i - sz.tiles, 0), 0, 0)
     )
-    total = sz.stride * sz.devices
-    return pl.pallas_call(
-        functools.partial(pack_kernel, sz),
-        grid=(sz.tiles + sz.devices // sz.dests,),
-        in_specs=[pl.BlockSpec(memory_space=pltpu.SMEM), tile, tile, tile],
-        out_specs=[piece, piece],
-        out_shape=[jax.ShapeDtypeStruct((sz.devices, sz.piece, LANES), jnp.int32)] * 2,
+    pieces = jax.ShapeDtypeStruct((sz.devices, sz.piece, LANES), jnp.int32)
+    places = pltpu.VMEM((sz.stride * sz.devices, LANES), jnp.int32)
+    grid = (sz.tiles + sz.devices // sz.dests,)
+    first, other, meta = pl.pallas_call(
+        functools.partial(pack_first_kernel, sz),
+        grid=grid,
+        in_specs=[pl.BlockSpec(lines, lambda i: (0, 0)), tile, tile, tile],
+        out_specs=[piece, tile, pl.BlockSpec(memory_space=pl.ANY)],
+        out_shape=[
+            pieces,
+            jax.ShapeDtypeStruct((sz.rows, LANES), jnp.int32),
+            jax.ShapeDtypeStruct(lines, jnp.int32),
+        ],
         scratch_shapes=[
-            pltpu.VMEM((2, total, LANES), jnp.int32),
-            pltpu.VMEM((sz.tile_rows, LANES), jnp.int32),
-            pltpu.VMEM((sz.tile_rows, LANES), jnp.int32),
+            places,
+            pltpu.SMEM(lines, jnp.int32),
+            pltpu.VMEM(lines, jnp.int32),
+            pltpu.VMEM((sz.seg, LANES), jnp.int32),
+            pltpu.VMEM((sz.seg, LANES), jnp.int32),
+            pltpu.SemaphoreType.DMA((2,)),
         ],
-        name="pack_rows",
-    )(meta, master, moment, second)
+        name="pack_first",
+    )(source_block.reshape(lines), master, moment, second)
+    other = pl.pallas_call(
+        functools.partial(pack_other_kernel, sz),
+        grid=grid,
+        in_specs=[pl.BlockSpec(memory_space=pltpu.SMEM), tile],
+        out_specs=piece,
+        out_shape=pieces,
+        scratch_shapes=[places],
+        cost_estimate=cost(25, 16 * LANES * sz.rows),
+        name="pack_other",
+    )(meta, other)
+    return first, other
 
 
 def place_call(sz, half, words, gradient):
-    sources = sz.devices // sz.dests
+    sources = sz.devices // sz.sources
     count = sz.w_tile * sz.w_blocks
     early = lambda i: jnp.minimum(i, sources - 1)
     late = lambda i: jnp.maximum(i - sources, 0)
@@ -382,11 +458,11 @@
         grid=(sources + sz.w_tiles,),
         in_specs=[
             pl.BlockSpec(
-                (sz.dests, 8, LANES),
+                (sz.sources, 8, LANES),
                 lambda i: (early(i), sz.slot_tile, 0),
                 memory_space=pltpu.SMEM,
             ),
-            pl.BlockSpec((sz.dests, sz.piece, LANES), lambda i: (early(i), 0, 0)),
+            pl.BlockSpec((sz.sources, sz.piece, LANES), lambda i: (early(i), 0, 0)),
             pl.BlockSpec((count, LANES), lambda i: (late(i), 0)),
         ],
         out_specs=[
@@ -400,10 +476,10 @@
         scratch_shapes=[
             pltpu.VMEM((sz.rows + 8, LANES), jnp.int32),
             pltpu.VMEM((sz.stride, LANES), jnp.int32),
+            pltpu.VMEM((sz.stride, LANES), jnp.int32),
             pltpu.VMEM((count, LANES), jnp.float32),
         ],
         cost_estimate=cost(25, 16 * LANES * sz.rows),
-        name=f"place_rows_{half}",
     )(words, words, gradient)
 
 
@@ -423,7 +499,7 @@
 
 def join_call(sz, first, other):
     total = sz.w_rows * sz.n_tensor
-    n = next(k for k in (32, 16, 8, total) if total % k == 0)
+    n = next(k for k in (96, 64, 32, 16, 8, total) if total % k == 0)
     return pl.pallas_call(
         join_kernel,
         grid=(total // n,),
@@ -438,8 +514,7 @@
     n_dp = lax.axis_size("dp")
     n_tensor = lax.axis_size("tensor")
     sz = Sizes(master.shape[0], n_dp * n_tensor, n_tensor)
-    meta = index_call(sz, source_block)
-    sent = pack_call(sz, meta, master, moment, second)
+    sent = pack_calls(sz, source_block, master, moment, second)
     halves, kept = [], []
     for half in range(2):
         words = lax.all_to_all(

time: 398 us -> 388 us (0.975)
  Pallas kernels: 155 us -> 146 us
    pallas_call x2, Pallas kernels: 59.1 us -> 46.3 us  [place_call(): pl.pallas_call(functools.partial(place_kernel, sz, half), grid=(sources +...]
    pallas_call x2, Pallas kernels: 40.1 us -> 51.3 us  [the longest x1 32.3 us: pack_calls(): pl.pallas_call(functools.partial(pack_first_kernel, sz), grid=grid, in_sp...]
    pallas_call x1, Pallas kernels: 28.2 us -> 19.7 us  [join_call(): pl.pallas_call(join_kernel, grid=(total // n,), in_specs=[pl.BlockSpec((n...]
  transfers between devices with their start and end apart: 2 -> 2, of which waited for: 1 -> 1; matrix products, arithmetic and copies ran while one was open for 0% -> 0% of each run, Pallas kernels for 14% -> 18%
where the time goes in v3:
time: 388 us; the launch traced here: 387 us
  blocking collectives  193 us (50%)
  Pallas kernels  146 us (38%)
  waiting for transfers between devices  34.2 us (9%)
  between operations  14 us (4%)
    all_to_all x2, blocking collectives, per_device(): lax.all_to_all(sent[half], ('dp', 'tensor'), split_axis=0, concat_axis=0,...  193 us
    pallas_call x2, Pallas kernels, place_call(): pl.pallas_call(functools.partial(place_kernel, sz, half), grid=(sources +...  46.3 us
    all_gather x2, waiting for transfers between devices, per_device(): halves.append(lax.all_gather(rows, 'tensor', axis=0, tiled=True))  34.2 us
    pallas_call x1, Pallas kernels, pack_calls(): pl.pallas_call(functools.partial(pack_first_kernel, sz), grid=grid, in_sp...  32.3 us
    pallas_call x1, Pallas kernels, state_call(): pl.pallas_call(state_kernel, grid=(sz.rows // n,), in_specs=[tile] * 3, o...  28.8 us
    pallas_call x1, Pallas kernels, join_call(): pl.pallas_call(join_kernel, grid=(total // n,), in_specs=[pl.BlockSpec((n...  19.7 us
    pallas_call x1, Pallas kernels, pack_calls(): pl.pallas_call(functools.partial(pack_other_kernel, sz), grid=grid, in_sp...  19 us
  transfers between devices with their start and end apart: 2, of which 1 were waited for; matrix products, arithmetic and copies ran while one was open for 0% of the time, Pallas kernels for 18%

profile of v3, /device:TPU:0, one launch (start us, length us, event | category | flops | bytes accessed | tf_op | source)
XLA Modules:
  0.0 387.3 jit_solution(4700250223803830777)
XLA Ops:
  7.2 0.0 all-gather.3.cloned.1.call-start
  7.2 32.3 %pack_first.1 = (s32[32,248,128]{2,1,0:T(8,128)}, s32[10368,128]{1,0:T(8,128)}, s32[81,128]{1,0:T(8,128)}) custom-call(s32[81,128]{1,0:T(8,128)} %bitcast.1, f32[10368,128]{1,0:T(8,128)} %master.1, f32[10368,128]{1,0:T(8,128)} %moment.1, f32[10368,128]{1,0:T(8,128)} %second.1), custom_call_target="tpu_custom_call" | custom-call | tf_op jit(solution)/shard_map/pack_first/pallas_call | solution.py:418
  39.5 98.3 %all_to_all.10.slots.words = s32[32,248,128]{2,1,0:T(8,128)} all-to-all(s32[32,248,128]{2,1,0:T(8,128)} %get-tuple-element.14), channel_id=1, replica_groups=mesh['dp'=4,'tensor'=8] {'dp','tensor'}, dimensions={0} | all-to-all | bytes 8126464 | tf_op jit(solution)/shard_map/all_to_all | solution.py:520
  137.8 23.1 %shard_map.84 = (bf16[72,9216]{1,0:T(8,128)(2,1)}, s32[10368,128]{1,0:T(8,128)}) custom-call(s32[32,248,128]{2,1,0:T(8,128)} %all_to_all.10.slots.words, s32[32,248,128]{2,1,0:T(8,128)} %all_to_all.10.slots.words, bf16[10368,128]{1,0:T(8,128)(2,1)} %grad.5), custom_call_target="tpu_custom_call" | custom-call | flops 24999999488 | bytes 21233664 | tf_op jit(solution)/shard_map/pallas_call | solution.py:456
  160.9 0.0 all-gather.3.cloned.1.call-update
  160.9 0.0 all-gather.5.cloned.1.call-start
  161.0 19.0 %pack_other.1 = s32[32,248,128]{2,1,0:T(8,128)} custom-call(s32[81,128]{1,0:T(8,128)} %get-tuple-element.16.meta, s32[10368,128]{1,0:T(8,128)} %get-tuple-element.17.words), custom_call_target="tpu_custom_call" | custom-call | flops 24999999488 | bytes 21233664 | tf_op jit(solution)/shard_map/pack_other/pallas_call | solution.py:438
  179.9 94.6 %all_to_all.11.slots.words = s32[32,248,128]{2,1,0:T(8,128)} all-to-all(s32[32,248,128]{2,1,0:T(8,128)} %pack_other.1), channel_id=1, replica_groups=mesh['dp'=4,'tensor'=8] {'dp','tensor'}, dimensions={0} | all-to-all | bytes 8126464 | tf_op jit(solution)/shard_map/all_to_all | solution.py:520
  274.5 23.2 %shard_map.85 = (bf16[72,9216]{1,0:T(8,128)(2,1)}, s32[10368,128]{1,0:T(8,128)}) custom-call(s32[32,248,128]{2,1,0:T(8,128)} %all_to_all.11.slots.words, s32[32,248,128]{2,1,0:T(8,128)} %all_to_all.11.slots.words, bf16[10368,128]{1,0:T(8,128)(2,1)} %grad.5), custom_call_target="tpu_custom_call" | custom-call | flops 24999999488 | bytes 21233664 | tf_op jit(solution)/shard_map/pallas_call | solution.py:456
  297.7 0.0 all-gather.5.cloned.1.call-update
  297.7 28.8 %state_rows.1 = (f32[10368,128]{1,0:T(8,128)}, f32[10368,128]{1,0:T(8,128)}, f32[10368,128]{1,0:T(8,128)}) custom-call(s32[10368,128]{1,0:T(8,128)} %get-tuple-element.15.rows0, s32[10368,128]{1,0:T(8,128)} %get-tuple-element.18.rows1, bf16[10368,128]{1,0:T(8,128)(2,1)} %grad.5), custom_call_target="tpu_custom_call" | custom-call | flops 15000000512 | bytes 29196288 | tf_op jit(solution)/shard_map/state_rows/pallas_call | solution.py:489
  326.5 0.0 all-gather.3.cloned.1.call-done.first
  326.5 34.2 %all-gather.5.cloned.1.call-done.other = bf16[576,9216]{1,0:T(8,128)(2,1)} async-done(((bf16[72,9216]{1,0:T(8,128)(2,1)}), bf16[576,9216]{1,0:T(8,128)(2,1)}) %all-gather.5.cloned.1.call-update) | async-done | bytes 10616848 | tf_op jit(solution)/shard_map/all_gather | solution.py:525
  360.7 19.7 %join_halves.1 = bf16[576,18432]{1,0:T(8,128)(2,1)} custom-call(bf16[576,9216]{1,0:T(8,128)(2,1)} %all-gather.3.cloned.1.call-done.first, bf16[576,9216]{1,0:T(8,128)(2,1)} %all-gather.5.cloned.1.call-done.other), custom_call_target="tpu_custom_call" | custom-call | tf_op jit(solution)/shard_map/join_halves/pallas_call | solution.py:503
Async XLA Ops:
  7.2 319.4 %all-gather.3.cloned.1.call-start = ((), (), s32[]{:S(2)}) async-start(), calls=%async_computation.2 | async-start | bytes 11943936 | tf_op jit(solution)/shard_map/all_gather | solution.py:525
  160.9 199.8 %all-gather.5.cloned.1.call-start = ((), (), s32[]{:S(2)}) async-start(), calls=%async_computation.3 | async-start | bytes 11943936 | tf_op jit(solution)/shard_map/all_gather | solution.py:525
Sparse Core Ops, SparseCore 0:
  161.0 93.7 all-gather.2
  297.8 62.8 all-gather.4

commit v4 on v3

--- a/solution.py
+++ b/solution.py
@@ -97,7 +97,7 @@
         self.w_tile = next((n for n in (24, 16, 8) if self.w_rows % n == 0), self.w_rows)
         self.w_tiles = self.w_rows // self.w_tile
         assert self.stride * devices < 65536 and rows < 32768 and self.seg % 8 == 0
-        assert self.piece - 8 * self.slot_tile == 8 and self.w_blocks % 2 == 0
+        assert self.piece - 8 * self.slot_tile == 8 and self.w_blocks % 4 == 0
 
 
 def lane_of(shape):
@@ -295,7 +295,9 @@
     return master, moment, second
 
 
-def place_kernel(sz, half, slots, words, grad, weight, kept, rows, line, line_b, grad_f32):
+def place_kernel(
+    sz, half, slots, words, grad, weight_a, weight_b, kept, rows, line, line_b, grad_f32
+):
     step = pl.program_id(0)
     sources = sz.devices // sz.sources
 
@@ -345,12 +347,13 @@
         kept[...] = rows[pl.ds(base, count), :]
         grad_f32[...] = grad[...].astype(jnp.float32)
         low = lane_of((sz.w_tile, LANES)) < HALF
-        unroll = next(n for n in (4, 3, 2, 1) if (sz.w_blocks // 2) % n == 0)
-
-        def body(i, carry):
+        per_part = sz.w_blocks // 4
+        unroll = next(n for n in (4, 3, 2, 1) if per_part % n == 0)
+
+        def body(part, weight, i, carry):
             loaded = []
             for u in range(unroll):
-                c = i * unroll + u
+                c = part * per_part + i * unroll + u
                 loaded.append(
                     tuple(
                         ref[pl.ds(first + 2 * c + odd, sz.w_tile, stride=sz.w_blocks), :]
@@ -370,7 +373,8 @@
                 weight[:, pl.ds(at, LANES)] = new.astype(jnp.bfloat16)
             return carry
 
-        lax.fori_loop(0, sz.w_blocks // 2 // unroll, body, 0)
+        for part, weight in enumerate((weight_a, weight_b)):
+            lax.fori_loop(0, per_part // unroll, functools.partial(body, part, weight), 0)
 
 
 def state_kernel(rows0, rows1, grad, master_out, moment_out, second_out):
@@ -387,9 +391,9 @@
     lax.fori_loop(0, n // some, body, 0)
 
 
-def join_kernel(first, other, weight):
+def join_tile(first, other, weight):
     blocks = first.shape[1] // LANES
-    unroll = next(n for n in (8, 6, 4, 3, 2, 1) if blocks % n == 0)
+    unroll = next(n for n in (12, 9, 8, 6, 4, 3, 2, 1) if blocks % n == 0)
     low = lane_of((first.shape[0], LANES)) < HALF
 
     def body(i, carry):
@@ -404,6 +408,16 @@
         return carry
 
     lax.fori_loop(0, blocks // unroll, body, 0)
+
+
+def join_kernel(sz, count, shards, *refs):
+    firsts, others, weight = refs[:count], refs[count : 2 * count], refs[-1]
+    piece = pl.program_id(0) // sz.w_tiles
+    for q in range(count):
+
+        @pl.when(piece == q)
+        def _(q=q):
+            join_tile(firsts[q], others[q], weight)
 
 
 def pack_calls(sz, source_block, master, moment, second):
@@ -466,11 +480,13 @@
             pl.BlockSpec((count, LANES), lambda i: (late(i), 0)),
         ],
         out_specs=[
-            pl.BlockSpec((sz.w_tile, FF_WIN // 2), lambda i: (late(i), 0)),
+            pl.BlockSpec((sz.w_tile, FF_WIN // 4), lambda i: (late(i), 0)),
+            pl.BlockSpec((sz.w_tile, FF_WIN // 4), lambda i: (late(i), 0)),
             pl.BlockSpec((count, LANES), lambda i: (late(i), 0)),
         ],
         out_shape=[
-            jax.ShapeDtypeStruct((sz.w_rows, FF_WIN // 2), jnp.bfloat16),
+            jax.ShapeDtypeStruct((sz.w_rows, FF_WIN // 4), jnp.bfloat16),
+            jax.ShapeDtypeStruct((sz.w_rows, FF_WIN // 4), jnp.bfloat16),
             jax.ShapeDtypeStruct((sz.rows, LANES), jnp.int32),
         ],
         scratch_shapes=[
@@ -497,34 +513,103 @@
     )(rows0, rows1, gradient)
 
 
-def join_call(sz, first, other):
+def join_call(sz, keys, firsts, others, weight):
+    me = lax.axis_index("tensor")
+    count = len(keys)
+    where = jnp.stack([me ^ mask for mask, _ in keys]).astype(jnp.int32)
+    parts = [part for _, part in keys]
+
+    def place(i, shards):
+        piece = i // sz.w_tiles
+        part = sum(jnp.where(piece == q, p, 0) for q, p in enumerate(parts))
+        return shards[piece] * sz.w_tiles + i % sz.w_tiles, part
+
+    tiles = [
+        pl.BlockSpec(
+            (sz.w_tile, FF_WIN // 4),
+            lambda i, shards, q=q: (jnp.clip(i - q * sz.w_tiles, 0, sz.w_tiles - 1), 0),
+        )
+        for q in range(count)
+    ]
+    again = [] if weight is None else [weight]
+    return pl.pallas_call(
+        functools.partial(join_kernel, sz, count),
+        grid_spec=pltpu.PrefetchScalarGridSpec(
+            num_scalar_prefetch=1,
+            grid=(count * sz.w_tiles,),
+            in_specs=tiles + tiles + [pl.BlockSpec(memory_space=pl.ANY)] * len(again),
+            out_specs=pl.BlockSpec((sz.w_tile, FF_WIN // 2), place),
+        ),
+        out_shape=jax.ShapeDtypeStruct((sz.w_rows * sz.n_tensor, FF_WIN), jnp.bfloat16),
+        input_output_aliases={1 + 2 * count: 0} if again else {},
+        cost_estimate=cost(2 * count, 8 * count * sz.w_rows * FF_WIN // 4),
+    )(where, *firsts, *others, *again)
+
+
+def whole_join_call(sz, first, other):
     total = sz.w_rows * sz.n_tensor
     n = next(k for k in (96, 64, 32, 16, 8, total) if total % k == 0)
     return pl.pallas_call(
-        join_kernel,
+        join_tile,
         grid=(total // n,),
         in_specs=[pl.BlockSpec((n, FF_WIN // 2), lambda i: (i, 0))] * 2,
         out_specs=pl.BlockSpec((n, FF_WIN), lambda i: (i, 0)),
         out_shape=jax.ShapeDtypeStruct((total, FF_WIN), jnp.bfloat16),
-        name="join_halves",
+        name="join_whole",
     )(first, other)
+
+
+def hop(sz, value, bits):
+    pairs = [(i, i ^ bits) for i in range(sz.n_tensor)]
+    return lax.ppermute(value, "tensor", pairs)
+
+
+def spread(sz, own):
+    n = sz.n_tensor
+    got = {(0, part): own[part] for part in range(2)}
+    if n == 8:
+        for mask, part in ((2, 0), (4, 1), (2, 1), (4, 0)):
+            got[mask, part] = hop(sz, own[part], mask)
+        got[6, 0] = hop(sz, got[2, 0], 4)
+        got[6, 1] = hop(sz, got[4, 1], 2)
+    else:
+        for mask in range(2, n, 2):
+            for part in range(2):
+                got[mask, part] = hop(sz, own[part], mask)
+    for (mask, part), value in list(got.items()):
+        got[mask | 1, part] = hop(sz, value, 1)
+    return got
 
 
 def per_device(master, moment, second, gradient, source_block):
     n_dp = lax.axis_size("dp")
     n_tensor = lax.axis_size("tensor")
     sz = Sizes(master.shape[0], n_dp * n_tensor, n_tensor)
+    by_hops = sz.w_rows % 8 == 0 and n_tensor & (n_tensor - 1) == 0
     sent = pack_calls(sz, source_block, master, moment, second)
     halves, kept = [], []
     for half in range(2):
         words = lax.all_to_all(
             sent[half], ("dp", "tensor"), split_axis=0, concat_axis=0, tiled=True
         )
-        rows, words = place_call(sz, half, words, gradient)
+        *own, words = place_call(sz, half, words, gradient)
         kept.append(words)
-        halves.append(lax.all_gather(rows, "tensor", axis=0, tiled=True))
+        if by_hops:
+            halves.append(spread(sz, own))
+        else:
+            halves.append(lax.all_gather(jnp.concatenate(own, 1), "tensor", axis=0, tiled=True))
     outs = state_call(sz, kept[0], kept[1], gradient)
-    weight = join_call(sz, *halves)
+    if not by_hops:
+        return (*outs, whole_join_call(sz, *halves))
+    weight = None
+    masks = range(0, n_tensor, 2)
+    near = [m for m in masks if m & (m - 1) == 0]
+    far = [m for m in masks if m & (m - 1)]
+    groups = [[0, 1], near[1:], [m | 1 for m in near[1:]], far, [m | 1 for m in far]]
+    for group in groups:
+        keys = [(mask, part) for mask in group for part in range(2)]
+        firsts, others = ([half[key] for key in keys] for half in halves)
+        weight = join_call(sz, keys, firsts, others, weight)
     return (*outs, weight)
 
 

time: 388 us -> 419 us (1.080)
  blocking collectives: 193 us -> 98.2 us
  waiting for transfers between devices: 34.2 us -> 117 us
  Pallas kernels: 146 us -> 175 us
  starting transfers between devices: 0.08 us -> 20.7 us
  between operations: 14 us -> 0.75 us
    all_to_all x2 -> x1, blocking collectives: 193 us -> 98.2 us  [per_device(): lax.all_to_all(sent[half], ('dp', 'tensor'), split_axis=0, concat_axis=0,...]
    all_to_all x0 -> x1, waiting for transfers between devices: none -> 67.2 us  [per_device(): lax.all_to_all(sent[half], ('dp', 'tensor'), split_axis=0, concat_axis=0,...]
    ppermute x0 -> x28, waiting for transfers between devices: none -> 49.4 us  [hop(): return lax.ppermute(value, 'tensor', pairs)]
    all_gather x2 -> x0, waiting for transfers between devices: 34.2 us -> none  [per_device(): halves.append(lax.all_gather(rows, 'tensor', axis=0, tiled=True))]
    pallas_call x1 -> x5, Pallas kernels: 19.7 us -> 48.8 us  [join_call(): pl.pallas_call(functools.partial(join_kernel, sz, count), grid_spec=pltpu...]
    ppermute x0 -> x28, starting transfers between devices: none -> 16.9 us  [hop(): return lax.ppermute(value, 'tensor', pairs)]
  transfers between devices with their start and end apart: 2 -> 29, of which waited for: 1 -> 7; matrix products, arithmetic and copies ran while one was open for 0% -> 1% of each run, Pallas kernels for 18% -> 28%
where the time goes in v4:
time: 419 us; the launch traced here: 418 us
  Pallas kernels  175 us (42%)
  waiting for transfers between devices  117 us (28%)
  blocking collectives  98.2 us (23%)
  starting transfers between devices  20.7 us (5%)
    all_to_all x1, blocking collectives, per_device(): lax.all_to_all(sent[half], ('dp', 'tensor'), split_axis=0, concat_axis=0,...  98.2 us
    all_to_all x1, waiting for transfers between devices, per_device(): lax.all_to_all(sent[half], ('dp', 'tensor'), split_axis=0, concat_axis=0,...  67.2 us
    ppermute x28, waiting for transfers between devices, hop(): return lax.ppermute(value, 'tensor', pairs)  49.4 us
    pallas_call x5, Pallas kernels, join_call(): pl.pallas_call(functools.partial(join_kernel, sz, count), grid_spec=pltpu...  48.8 us
    pallas_call x2, Pallas kernels, place_call(): pl.pallas_call(functools.partial(place_kernel, sz, half), grid=(sources +...  46.2 us
    pallas_call x1, Pallas kernels, pack_calls(): pl.pallas_call(functools.partial(pack_first_kernel, sz), grid=grid, in_sp...  32.3 us
    pallas_call x1, Pallas kernels, state_call(): pl.pallas_call(state_kernel, grid=(sz.rows // n,), in_specs=[tile] * 3, o...  29 us
    pallas_call x1, Pallas kernels, pack_calls(): pl.pallas_call(functools.partial(pack_other_kernel, sz), grid=grid, in_sp...  19 us
  transfers between devices with their start and end apart: 29, of which 7 were waited for; matrix products, arithmetic and copies ran while one was open for 1% of the time, Pallas kernels for 28%

profile of v4, /device:TPU:0, one launch (start us, length us, event | category | flops | bytes accessed | tf_op | source)
XLA Modules:
  0.0 417.7 jit_solution(18194202189355326923)
XLA Ops:
  0.6 32.3 %pack_first.1 = (s32[32,248,128]{2,1,0:T(8,128)}, s32[10368,128]{1,0:T(8,128)}, s32[81,128]{1,0:T(8,128)}) custom-call(s32[81,128]{1,0:T(8,128)} %bitcast.9, f32[10368,128]{1,0:T(8,128)} %master.1, f32[10368,128]{1,0:T(8,128)} %moment.1, f32[10368,128]{1,0:T(8,128)} %second.1), custom_call_target="tpu_custom_call" | custom-call | tf_op jit(solution)/shard_map/pack_first/pallas_call | solution.py:432
  33.0 19.0 %pack_other.1 = s32[32,248,128]{2,1,0:T(8,128)} custom-call(s32[81,128]{1,0:T(8,128)} %get-tuple-element.18.meta, s32[10368,128]{1,0:T(8,128)} %get-tuple-element.19.words), custom_call_target="tpu_custom_call" | custom-call | flops 24999999488 | bytes 21233664 | tf_op jit(solution)/shard_map/pack_other/pallas_call | solution.py:452
  51.9 98.2 %all_to_all.10.slots.words = s32[32,248,128]{2,1,0:T(8,128)} all-to-all(s32[32,248,128]{2,1,0:T(8,128)} %pack_other.1), channel_id=1, replica_groups=mesh['dp'=4,'tensor'=8] {'dp','tensor'}, dimensions={0} | all-to-all | bytes 8126464 | tf_op jit(solution)/shard_map/all_to_all | solution.py:592
  150.2 3.8 all-to-all-start
  154.0 23.1 %shard_map.85 = (bf16[72,4608]{1,0:T(8,128)(2,1)}, bf16[72,4608]{1,0:T(8,128)(2,1)}, s32[10368,128]{1,0:T(8,128)}) custom-call(s32[32,248,128]{2,1,0:T(8,128)} %all_to_all.10.slots.words, s32[32,248,128]{2,1,0:T(8,128)} %all_to_all.10.slots.words, bf16[10368,128]{1,0:T(8,128)(2,1)} %grad.5), custom_call_target="tpu_custom_call" | custom-call | flops 24999999488 | bytes 21233664 | tf_op jit(solution)/shard_map/pallas_call | solution.py:470
  177.6 67.2 %all-to-all-done.slots.words = s32[32,248,128]{2,1,0:T(8,128)} async-done(((s32[32,248,128]{2,1,0:T(8,128)}), s32[32,248,128]{2,1,0:T(8,128)}, u32[]{:S(2)}, u32[]{:S(2)}) %all-to-all-start) | async-done | bytes 4063264 | tf_op jit(solution)/shard_map/all_to_all | solution.py:592
  244.8 23.1 %shard_map.84 = (bf16[72,4608]{1,0:T(8,128)(2,1)}, bf16[72,4608]{1,0:T(8,128)(2,1)}, s32[10368,128]{1,0:T(8,128)}) custom-call(s32[32,248,128]{2,1,0:T(8,128)} %all-to-all-done.slots.words, s32[32,248,128]{2,1,0:T(8,128)} %all-to-all-done.slots.words, bf16[10368,128]{1,0:T(8,128)(2,1)} %grad.5), custom_call_target="tpu_custom_call" | custom-call | flops 24999999488 | bytes 21233664 | tf_op jit(solution)/shard_map/pallas_call | solution.py:470
  268.4 1.4 collective-permute-start.6
  269.9 1.6 collective-permute-start.9
  273.4 1.4 collective-permute-start
  277.9 8.6 %collective-permute-done.6.refs_4_ = bf16[72,4608]{1,0:T(8,128)(2,1)S(1)} collective-permute-done((bf16[72,4608]{1,0:T(8,128)(2,1)}, bf16[72,4608]{1,0:T(8,128)(2,1)S(1)}, u32[]{:S(2)}, u32[]{:S(2)}) %collective-permute-start.6) | collective-permute-done | bytes 663584 | tf_op jit(solution)/shard_map/ppermute | solution.py:564
  287.9 1.6 collective-permute-start.13
  289.4 11.2 %collective-permute-done.19.refs_5_ = bf16[72,4608]{1,0:T(8,128)(2,1)S(1)} collective-permute-done((bf16[72,4608]{1,0:T(8,128)(2,1)}, bf16[72,4608]{1,0:T(8,128)(2,1)S(1)}, u32[]{:S(2)}, u32[]{:S(2)}) %collective-permute-start.19) | collective-permute-done | bytes 663584 | tf_op jit(solution)/shard_map/ppermute | solution.py:564
  302.1 12.8 %collective-permute-done.refs_0_ = bf16[72,4608]{1,0:T(8,128)(2,1)S(1)} collective-permute-done((bf16[72,4608]{1,0:T(8,128)(2,1)}, bf16[72,4608]{1,0:T(8,128)(2,1)S(1)}, u32[]{:S(2)}, u32[]{:S(2)}) %collective-permute-start) | collective-permute-done | bytes 663584 | tf_op jit(solution)/shard_map/ppermute | solution.py:564
  314.9 29.0 %state_rows.1 = (f32[10368,128]{1,0:T(8,128)}, f32[10368,128]{1,0:T(8,128)}, f32[10368,128]{1,0:T(8,128)}) custom-call(s32[10368,128]{1,0:T(8,128)} %get-tuple-element.17.rows0, s32[10368,128]{1,0:T(8,128)} %get-tuple-element.20.rows1, bf16[10368,128]{1,0:T(8,128)(2,1)} %grad.5), custom_call_target="tpu_custom_call" | custom-call | flops 15000000512 | bytes 29196288 | tf_op jit(solution)/shard_map/state_rows/pallas_call | solution.py:505
  345.3 11.7 %shard_map.86.refs_8_ = bf16[576,18432]{1,0:T(8,128)(2,1)} custom-call(s32[4]{0:T(128)} %pad_add_fusion.4.shards, bf16[72,4608]{1,0:T(8,128)(2,1)} %get-tuple-element.24.refs_0_, bf16[72,4608]{1,0:T(8,128)(2,1)} %get-tuple-element.25.refs_1_, bf16[72,4608]{1,0:T(8,128)(2,1)} %collective-permute-done.24.refs_2_, bf16[72,4608]{1,0:T(8,128)(2,1)} %copy-done.11, ...), custom_call_target="tpu_custom_call" | custom-call | flops 8000000000 | bytes 10616832 | tf_op jit(solution)/shard_map/pallas_call | solution.py:535
  357.0 1.5 collective-permute-start.10
  358.5 1.6 collective-permute-start.7
  361.1 11.7 %shard_map.87.refs_8_ = bf16[576,18432]{1,0:T(8,128)(2,1)} custom-call(s32[4]{0:T(128)} %pad_add_fusion.3.shards, bf16[72,4608]{1,0:T(8,128)(2,1)} %copy-done.2, bf16[72,4608]{1,0:T(8,128)(2,1)} %collective-permute-done.13.refs_1_, bf16[72,4608]{1,0:T(8,128)(2,1)} %collective-permute-done.15.refs_2_, ...), custom_call_target="tpu_custom_call", output_to_operand_aliasing={{}: (9, {})} | custom-call | flops 8000000000 | bytes 10616832 | tf_op jit(solution)/shard_map/pallas_call | solution.py:535
  372.8 2.1 collective-permute-done.10.refs_3_
  376.3 13.3 %collective-permute-done.1.refs_0_ = bf16[72,4608]{1,0:T(8,128)(2,1)} collective-permute-done((bf16[72,4608]{1,0:T(8,128)(2,1)S(1)}, bf16[72,4608]{1,0:T(8,128)(2,1)}, u32[]{:S(2)}, u32[]{:S(2)}) %collective-permute-start.1) | collective-permute-done | bytes 663584 | tf_op jit(solution)/shard_map/ppermute | solution.py:564
  391.0 11.7 %shard_map.88.refs_4_ = bf16[576,18432]{1,0:T(8,128)(2,1)} custom-call(s32[4]{0:T(128)} %pad_add_fusion.2.shards, bf16[72,4608]{1,0:T(8,128)(2,1)} %collective-permute-done.12.refs_0_, bf16[72,4608]{1,0:T(8,128)(2,1)} %collective-permute-done.14.refs_1_, bf16[72,4608]{1,0:T(8,128)(2,1)} %copy-done.5, ...), custom_call_target="tpu_custom_call", output_to_operand_aliasing={{}: (9, {})} | custom-call | flops 8000000000 | bytes 10616832 | tf_op jit(solution)/shard_map/pallas_call | solution.py:535
  402.6 6.9 %shard_map.89.refs_4_ = bf16[576,18432]{1,0:T(8,128)(2,1)} custom-call(s32[2]{0:T(128)} %pad_add_fusion.1.shards, bf16[72,4608]{1,0:T(8,128)(2,1)} %collective-permute-done.1.refs_0_, bf16[72,4608]{1,0:T(8,128)(2,1)} %collective-permute-done.4.refs_1_, bf16[72,4608]{1,0:T(8,128)(2,1)} %copy-done.6, ...), custom_call_target="tpu_custom_call", output_to_operand_aliasing={{}: (5, {})} | custom-call | flops 4000000000 | bytes 5308416 | tf_op jit(solution)/shard_map/pallas_call | solution.py:535
  410.8 6.9 %shard_map.90 = bf16[576,18432]{1,0:T(8,128)(2,1)} custom-call(s32[2]{0:T(128)} %pad_add_fusion.shards, bf16[72,4608]{1,0:T(8,128)(2,1)} %copy-done.9, bf16[72,4608]{1,0:T(8,128)(2,1)} %collective-permute-done.5.refs_1_, bf16[72,4608]{1,0:T(8,128)(2,1)} %copy-done.8, bf16[72,4608]{1,0:T(8,128)(2,1)} %copy-done.7, ...), custom_call_target="tpu_custom_call", output_to_operand_aliasing={{}: (5, {})} | custom-call | flops 4000000000 | bytes 5308416 | tf_op jit(solution)/shard_map/pallas_call | solution.py:535
  (74 shorter events, 15.2 us)
Async XLA Ops:
  150.2 94.7 %all-to-all-start = ((s32[32,248,128]{2,1,0:T(8,128)}), s32[32,248,128]{2,1,0:T(8,128)}, u32[]{:S(2)}, u32[]{:S(2)}) async-start(s32[32,248,128]{2,1,0:T(8,128)} %get-tuple-element.16), calls=%async_computation | async-start | bytes 8126464 | tf_op jit(solution)/shard_map/all_to_all | solution.py:592
  177.1 92.8 %collective-permute-start.26 = (bf16[72,4608]{1,0:T(8,128)(2,1)}, bf16[72,4608]{1,0:T(8,128)(2,1)}, u32[]{:S(2)}, u32[]{:S(2)}) collective-permute-start(bf16[72,4608]{1,0:T(8,128)(2,1)} %get-tuple-element.26.refs_4_), channel_id=1, source_target_pairs={{0,1},{1,0},{2,3},{3,2},{4,5},{5,4},{6,7},{7,6},{8,9},{9,8},{10,11... | collective-permute-start | bytes 1990664 | tf_op jit(solution)/shard_map/ppermute | solution.py:564
  177.3 94.2 %collective-permute-start.27 = (bf16[72,4608]{1,0:T(8,128)(2,1)}, bf16[72,4608]{1,0:T(8,128)(2,1)S(1)}, u32[]{:S(2)}, u32[]{:S(2)}) collective-permute-start(bf16[72,4608]{1,0:T(8,128)(2,1)} %get-tuple-element.27.refs_5_), channel_id=1, source_target_pairs={{0,1},{1,0},{2,3},{3,2},{4,5},{5,4},{6,7},{7,6},{8,9},{9,8},{10,11... | collective-permute-start | bytes 1990664 | tf_op jit(solution)/shard_map/ppermute | solution.py:564
  268.4 18.0 %collective-permute-start.6 = (bf16[72,4608]{1,0:T(8,128)(2,1)}, bf16[72,4608]{1,0:T(8,128)(2,1)S(1)}, u32[]{:S(2)}, u32[]{:S(2)}) collective-permute-start(bf16[72,4608]{1,0:T(8,128)(2,1)} %get-tuple-element.26.refs_4_), channel_id=1, source_target_pairs={{0,2},{1,3},{2,0},{3,1},{4,6},{5,7},{6,4},{7,5},{8,10},{9,11},{10,... | collective-permute-start | bytes 1990664 | tf_op jit(solution)/shard_map/ppermute | solution.py:564
  269.9 18.0 %collective-permute-start.9 = (bf16[72,4608]{1,0:T(8,128)(2,1)}, bf16[72,4608]{1,0:T(8,128)(2,1)S(1)}, u32[]{:S(2)}, u32[]{:S(2)}) collective-permute-start(bf16[72,4608]{1,0:T(8,128)(2,1)} %get-tuple-element.27.refs_5_), channel_id=1, source_target_pairs={{0,4},{1,5},{2,6},{3,7},{4,0},{5,1},{6,2},{7,3},{8,12},{9,13},{10,... | collective-permute-start | bytes 1990664 | tf_op jit(solution)/shard_map/ppermute | solution.py:564
  271.5 29.2 %collective-permute-start.19 = (bf16[72,4608]{1,0:T(8,128)(2,1)}, bf16[72,4608]{1,0:T(8,128)(2,1)S(1)}, u32[]{:S(2)}, u32[]{:S(2)}) collective-permute-start(bf16[72,4608]{1,0:T(8,128)(2,1)} %get-tuple-element.27.refs_5_), channel_id=1, source_target_pairs={{0,2},{1,3},{2,0},{3,1},{4,6},{5,7},{6,4},{7,5},{8,10},{9,11},{10,... | collective-permute-start | bytes 1990664 | tf_op jit(solution)/shard_map/ppermute | solution.py:564
  271.9 30.2 %collective-permute-start.21 = (bf16[72,4608]{1,0:T(8,128)(2,1)}, bf16[72,4608]{1,0:T(8,128)(2,1)S(1)}, u32[]{:S(2)}, u32[]{:S(2)}) collective-permute-start(bf16[72,4608]{1,0:T(8,128)(2,1)} %get-tuple-element.26.refs_4_), channel_id=1, source_target_pairs={{0,4},{1,5},{2,6},{3,7},{4,0},{5,1},{6,2},{7,3},{8,12},{9,13},{10,... | collective-permute-start | bytes 1990664 | tf_op jit(solution)/shard_map/ppermute | solution.py:564
  273.4 41.4 %collective-permute-start = (bf16[72,4608]{1,0:T(8,128)(2,1)}, bf16[72,4608]{1,0:T(8,128)(2,1)S(1)}, u32[]{:S(2)}, u32[]{:S(2)}) collective-permute-start(bf16[72,4608]{1,0:T(8,128)(2,1)} %get-tuple-element.24.refs_0_), channel_id=1, source_target_pairs={{0,2},{1,3},{2,0},{3,1},{4,6},{5,7},{6,4},{7,5},{8,10},{9,11},{10,... | collective-permute-start | bytes 1990664 | tf_op jit(solution)/shard_map/ppermute | solution.py:564
  286.4 57.5 %collective-permute-start.3 = (bf16[72,4608]{1,0:T(8,128)(2,1)}, bf16[72,4608]{1,0:T(8,128)(2,1)}, u32[]{:S(2)}, u32[]{:S(2)}) collective-permute-start(bf16[72,4608]{1,0:T(8,128)(2,1)} %get-tuple-element.25.refs_1_), channel_id=1, source_target_pairs={{0,4},{1,5},{2,6},{3,7},{4,0},{5,1},{6,2},{7,3},{8,12},{9,13},{10,... | collective-permute-start | bytes 1990664 | tf_op jit(solution)/shard_map/ppermute | solution.py:564
  287.9 56.4 %collective-permute-start.13 = (bf16[72,4608]{1,0:T(8,128)(2,1)}, bf16[72,4608]{1,0:T(8,128)(2,1)}, u32[]{:S(2)}, u32[]{:S(2)}) collective-permute-start(bf16[72,4608]{1,0:T(8,128)(2,1)} %get-tuple-element.25.refs_1_), channel_id=1, source_target_pairs={{0,2},{1,3},{2,0},{3,1},{4,6},{5,7},{6,4},{7,5},{8,10},{9,11},{10,... | collective-permute-start | bytes 1990664 | tf_op jit(solution)/shard_map/ppermute | solution.py:564
  300.7 43.9 %collective-permute-start.15 = (bf16[72,4608]{1,0:T(8,128)(2,1)}, bf16[72,4608]{1,0:T(8,128)(2,1)}, u32[]{:S(2)}, u32[]{:S(2)}) collective-permute-start(bf16[72,4608]{1,0:T(8,128)(2,1)} %get-tuple-element.24.refs_0_), channel_id=1, source_target_pairs={{0,4},{1,5},{2,6},{3,7},{4,0},{5,1},{6,2},{7,3},{8,12},{9,13},{10,... | collective-permute-start | bytes 1990664 | tf_op jit(solution)/shard_map/ppermute | solution.py:564
  302.1 42.7 %collective-permute-start.18 = (bf16[72,4608]{1,0:T(8,128)(2,1)S(1)}, bf16[72,4608]{1,0:T(8,128)(2,1)}, u32[]{:S(2)}, u32[]{:S(2)}) collective-permute-start(bf16[72,4608]{1,0:T(8,128)(2,1)S(1)} %collective-permute-done.6.refs_4_), channel_id=1, source_target_pairs={{0,1},{1,0},{2,3},{3,2},{4,5},{5,4},{6,7},{7,6},{8,9},{9,8},{10,11... | collective-permute-start | bytes 1990664 | tf_op jit(solution)/shard_map/ppermute | solution.py:564
  314.9 30.2 %collective-permute-start.23 = (bf16[72,4608]{1,0:T(8,128)(2,1)S(1)}, bf16[72,4608]{1,0:T(8,128)(2,1)}, u32[]{:S(2)}, u32[]{:S(2)}) collective-permute-start(bf16[72,4608]{1,0:T(8,128)(2,1)S(1)} %collective-permute-done.9.refs_7_), channel_id=1, source_target_pairs={{0,1},{1,0},{2,3},{3,2},{4,5},{5,4},{6,7},{7,6},{8,9},{9,8},{10,11... | collective-permute-start | bytes 1990664 | tf_op jit(solution)/shard_map/ppermute | solution.py:564
  344.8 15.7 %collective-permute-start.17 = (bf16[72,4608]{1,0:T(8,128)(2,1)}, bf16[72,4608]{1,0:T(8,128)(2,1)}, u32[]{:S(2)}, u32[]{:S(2)}) collective-permute-start(bf16[72,4608]{1,0:T(8,128)(2,1)} %collective-permute-done.3.refs_3_), channel_id=1, source_target_pairs={{0,1},{1,0},{2,3},{3,2},{4,5},{5,4},{6,7},{7,6},{8,9},{9,8},{10,11... | collective-permute-start | bytes 1990664 | tf_op jit(solution)/shard_map/ppermute | solution.py:564
  345.0 16.1 %collective-permute-start.14 = (bf16[72,4608]{1,0:T(8,128)(2,1)}, bf16[72,4608]{1,0:T(8,128)(2,1)}, u32[]{:S(2)}, u32[]{:S(2)}) collective-permute-start(bf16[72,4608]{1,0:T(8,128)(2,1)} %collective-permute-done.13.refs_1_), channel_id=1, source_target_pairs={{0,1},{1,0},{2,3},{3,2},{4,5},{5,4},{6,7},{7,6},{8,9},{9,8},{10,11... | collective-permute-start | bytes 1990664 | tf_op jit(solution)/shard_map/ppermute | solution.py:564
  357.0 18.0 %collective-permute-start.10 = (bf16[72,4608]{1,0:T(8,128)(2,1)S(1)}, bf16[72,4608]{1,0:T(8,128)(2,1)}, u32[]{:S(2)}, u32[]{:S(2)}) collective-permute-start(bf16[72,4608]{1,0:T(8,128)(2,1)S(1)} %collective-permute-done.9.refs_7_), channel_id=1, source_target_pairs={{0,2},{1,3},{2,0},{3,1},{4,6},{5,7},{6,4},{7,5},{8,10},{9,11},{10,... | collective-permute-start | bytes 1990664 | tf_op jit(solution)/shard_map/ppermute | solution.py:564
  358.5 17.8 %collective-permute-start.7 = (bf16[72,4608]{1,0:T(8,128)(2,1)S(1)}, bf16[72,4608]{1,0:T(8,128)(2,1)S(1)}, u32[]{:S(2)}, u32[]{:S(2)}) collective-permute-start(bf16[72,4608]{1,0:T(8,128)(2,1)S(1)} %collective-permute-done.6.refs_4_), channel_id=1, source_target_pairs={{0,4},{1,5},{2,6},{3,7},{4,0},{5,1},{6,2},{7,3},{8,12},{9,13},{10,... | collective-permute-start | bytes 1990664 | tf_op jit(solution)/shard_map/ppermute | solution.py:564
  360.1 29.5 %collective-permute-start.1 = (bf16[72,4608]{1,0:T(8,128)(2,1)S(1)}, bf16[72,4608]{1,0:T(8,128)(2,1)}, u32[]{:S(2)}, u32[]{:S(2)}) collective-permute-start(bf16[72,4608]{1,0:T(8,128)(2,1)S(1)} %collective-permute-done.refs_0_), channel_id=1, source_target_pairs={{0,4},{1,5},{2,6},{3,7},{4,0},{5,1},{6,2},{7,3},{8,12},{9,13},{10,... | collective-permute-start | bytes 1990664 | tf_op jit(solution)/shard_map/ppermute | solution.py:564
  360.5 29.1 %collective-permute-start.4 = (bf16[72,4608]{1,0:T(8,128)(2,1)}, bf16[72,4608]{1,0:T(8,128)(2,1)}, u32[]{:S(2)}, u32[]{:S(2)}) collective-permute-start(bf16[72,4608]{1,0:T(8,128)(2,1)} %collective-permute-done.3.refs_3_), channel_id=1, source_target_pairs={{0,2},{1,3},{2,0},{3,1},{4,6},{5,7},{6,4},{7,5},{8,10},{9,11},{10,... | collective-permute-start | bytes 1990664 | tf_op jit(solution)/shard_map/ppermute | solution.py:564
  361.1 29.0 %collective-permute-start.16 = (bf16[72,4608]{1,0:T(8,128)(2,1)}, bf16[72,4608]{1,0:T(8,128)(2,1)S(1)}, u32[]{:S(2)}, u32[]{:S(2)}) collective-permute-start(bf16[72,4608]{1,0:T(8,128)(2,1)} %collective-permute-done.15.refs_2_), channel_id=1, source_target_pairs={{0,1},{1,0},{2,3},{3,2},{4,5},{5,4},{6,7},{7,6},{8,9},{9,8},{10,11... | collective-permute-start | bytes 1990664 | tf_op jit(solution)/shard_map/ppermute | solution.py:564
  374.9 34.6 %collective-permute-start.11 = (bf16[72,4608]{1,0:T(8,128)(2,1)}, bf16[72,4608]{1,0:T(8,128)(2,1)S(1)}, u32[]{:S(2)}, u32[]{:S(2)}) collective-permute-start(bf16[72,4608]{1,0:T(8,128)(2,1)} %collective-permute-done.10.refs_3_), channel_id=1, source_target_pairs={{0,1},{1,0},{2,3},{3,2},{4,5},{5,4},{6,7},{7,6},{8,9},{9,8},{10,11... | collective-permute-start | bytes 1990664 | tf_op jit(solution)/shard_map/ppermute | solution.py:564
  376.3 33.3 %collective-permute-start.8 = (bf16[72,4608]{1,0:T(8,128)(2,1)S(1)}, bf16[72,4608]{1,0:T(8,128)(2,1)S(1)}, u32[]{:S(2)}, u32[]{:S(2)}) collective-permute-start(bf16[72,4608]{1,0:T(8,128)(2,1)S(1)} %collective-permute-done.7.refs_2_), channel_id=1, source_target_pairs={{0,1},{1,0},{2,3},{3,2},{4,5},{5,4},{6,7},{7,6},{8,9},{9,8},{10,11... | collective-permute-start | bytes 1990664 | tf_op jit(solution)/shard_map/ppermute | solution.py:564
  389.6 20.0 %collective-permute-start.2 = (bf16[72,4608]{1,0:T(8,128)(2,1)}, bf16[72,4608]{1,0:T(8,128)(2,1)S(1)}, u32[]{:S(2)}, u32[]{:S(2)}) collective-permute-start(bf16[72,4608]{1,0:T(8,128)(2,1)} %collective-permute-done.1.refs_0_), channel_id=1, source_target_pairs={{0,1},{1,0},{2,3},{3,2},{4,5},{5,4},{6,7},{7,6},{8,9},{9,8},{10,11... | collective-permute-start | bytes 1990664 | tf_op jit(solution)/shard_map/ppermute | solution.py:564
  389.6 20.0 %collective-permute-start.5 = (bf16[72,4608]{1,0:T(8,128)(2,1)}, bf16[72,4608]{1,0:T(8,128)(2,1)}, u32[]{:S(2)}, u32[]{:S(2)}) collective-permute-start(bf16[72,4608]{1,0:T(8,128)(2,1)} %collective-permute-done.4.refs_1_), channel_id=1, source_target_pairs={{0,1},{1,0},{2,3},{3,2},{4,5},{5,4},{6,7},{7,6},{8,9},{9,8},{10,11... | collective-permute-start | bytes 1990664 | tf_op jit(solution)/shard_map/ppermute | solution.py:564
  (17 other events, 355.5 us)

commit v5 on v4

--- a/solution.py
+++ b/solution.py
@@ -348,7 +348,7 @@
         grad_f32[...] = grad[...].astype(jnp.float32)
         low = lane_of((sz.w_tile, LANES)) < HALF
         per_part = sz.w_blocks // 4
-        unroll = next(n for n in (4, 3, 2, 1) if per_part % n == 0)
+        unroll = next(n for n in (12, 9, 6, 4, 3, 2, 1) if per_part % n == 0)
 
         def body(part, weight, i, carry):
             loaded = []
@@ -379,7 +379,7 @@
 
 def state_kernel(rows0, rows1, grad, master_out, moment_out, second_out):
     n = rows0.shape[0]
-    some = next(k for k in (64, 48, 32, 16) if n % k == 0)
+    some = next(k for k in (288, 144, 96, 48, 32, 16) if n % k == 0)
 
     def body(i, carry):
         at = pl.ds(pl.multiple_of(i * some, some), some)
@@ -410,12 +410,11 @@
     lax.fori_loop(0, blocks // unroll, body, 0)
 
 
-def join_kernel(sz, count, shards, *refs):
+def join_kernel(count, shards, *refs):
     firsts, others, weight = refs[:count], refs[count : 2 * count], refs[-1]
-    piece = pl.program_id(0) // sz.w_tiles
     for q in range(count):
 
-        @pl.when(piece == q)
+        @pl.when(pl.program_id(0) == q)
         def _(q=q):
             join_tile(firsts[q], others[q], weight)
 
@@ -500,7 +499,7 @@
 
 
 def state_call(sz, rows0, rows1, gradient):
-    n = sz.tile_rows if sz.tile_rows % 16 == 0 else sz.rows
+    n = next((k for k in (1728, 1296, 864, 432) if sz.rows % k == 0), sz.rows)
     tile = pl.BlockSpec((n, LANES), lambda i: (i, 0))
     return pl.pallas_call(
         state_kernel,
@@ -520,25 +519,17 @@
     parts = [part for _, part in keys]
 
     def place(i, shards):
-        piece = i // sz.w_tiles
-        part = sum(jnp.where(piece == q, p, 0) for q, p in enumerate(parts))
-        return shards[piece] * sz.w_tiles + i % sz.w_tiles, part
-
-    tiles = [
-        pl.BlockSpec(
-            (sz.w_tile, FF_WIN // 4),
-            lambda i, shards, q=q: (jnp.clip(i - q * sz.w_tiles, 0, sz.w_tiles - 1), 0),
-        )
-        for q in range(count)
-    ]
+        return shards[i], sum(jnp.where(i == q, p, 0) for q, p in enumerate(parts))
+
+    tiles = [pl.BlockSpec((sz.w_rows, FF_WIN // 4), lambda i, shards: (0, 0))] * count
     again = [] if weight is None else [weight]
     return pl.pallas_call(
-        functools.partial(join_kernel, sz, count),
+        functools.partial(join_kernel, count),
         grid_spec=pltpu.PrefetchScalarGridSpec(
             num_scalar_prefetch=1,
-            grid=(count * sz.w_tiles,),
+            grid=(count,),
             in_specs=tiles + tiles + [pl.BlockSpec(memory_space=pl.ANY)] * len(again),
-            out_specs=pl.BlockSpec((sz.w_tile, FF_WIN // 2), place),
+            out_specs=pl.BlockSpec((sz.w_rows, FF_WIN // 2), place),
         ),
         out_shape=jax.ShapeDtypeStruct((sz.w_rows * sz.n_tensor, FF_WIN), jnp.bfloat16),
         input_output_aliases={1 + 2 * count: 0} if again else {},

time: 419 us -> 390 us (0.931)
  Pallas kernels: 175 us -> 139 us
  waiting for transfers between devices: 117 us -> 124 us
    pallas_call x5, Pallas kernels: 48.8 us -> 31.7 us  [join_call(): pl.pallas_call(functools.partial(join_kernel, count), grid_spec=pltpu.Pre...]
    pallas_call x1, Pallas kernels: 29 us -> 16.6 us  [state_call(): pl.pallas_call(state_kernel, grid=(sz.rows // n,), in_specs=[tile] * 3, o...]
    pallas_call x2, Pallas kernels: 46.2 us -> 39.5 us  [place_call(): pl.pallas_call(functools.partial(place_kernel, sz, half), grid=(sources +...]
    ppermute x28, waiting for transfers between devices: 49.4 us -> 53.7 us  [hop(): return lax.ppermute(value, 'tensor', pairs)]
  transfers between devices with their start and end apart: 29 -> 29, of which waited for: 7 -> 7; matrix products, arithmetic and copies ran while one was open for 1% -> 1% of each run, Pallas kernels for 28% -> 21%
where the time goes in v5:
time: 390 us; the launch traced here: 389 us
  Pallas kernels  139 us (36%)
  waiting for transfers between devices  124 us (32%)
  blocking collectives  98.2 us (25%)
  starting transfers between devices  20.7 us (5%)
    all_to_all x1, blocking collectives, per_device(): lax.all_to_all(sent[half], ('dp', 'tensor'), split_axis=0, concat_axis=0,...  98.2 us
    all_to_all x1, waiting for transfers between devices, per_device(): lax.all_to_all(sent[half], ('dp', 'tensor'), split_axis=0, concat_axis=0,...  70.6 us
    ppermute x28, waiting for transfers between devices, hop(): return lax.ppermute(value, 'tensor', pairs)  53.7 us
    pallas_call x2, Pallas kernels, place_call(): pl.pallas_call(functools.partial(place_kernel, sz, half), grid=(sources +...  39.5 us
    pallas_call x1, Pallas kernels, pack_calls(): pl.pallas_call(functools.partial(pack_first_kernel, sz), grid=grid, in_sp...  32.3 us
    pallas_call x5, Pallas kernels, join_call(): pl.pallas_call(functools.partial(join_kernel, count), grid_spec=pltpu.Pre...  31.7 us
    pallas_call x1, Pallas kernels, pack_calls(): pl.pallas_call(functools.partial(pack_other_kernel, sz), grid=grid, in_sp...  19 us
    ppermute x28, starting transfers between devices, hop(): return lax.ppermute(value, 'tensor', pairs)  16.9 us
  transfers between devices with their start and end apart: 29, of which 7 were waited for; matrix products, arithmetic and copies ran while one was open for 1% of the time, Pallas kernels for 21%

profile of v5, /device:TPU:0, one launch (start us, length us, event | category | flops | bytes accessed | tf_op | source)
XLA Modules:
  0.0 389.0 jit_solution(7969875025888991918)
XLA Ops:
  0.6 32.3 %pack_first.1 = (s32[32,248,128]{2,1,0:T(8,128)}, s32[10368,128]{1,0:T(8,128)}, s32[81,128]{1,0:T(8,128)}) custom-call(s32[81,128]{1,0:T(8,128)} %bitcast.9, f32[10368,128]{1,0:T(8,128)} %master.1, f32[10368,128]{1,0:T(8,128)} %moment.1, f32[10368,128]{1,0:T(8,128)} %second.1), custom_call_target="tpu_custom_call" | custom-call | tf_op jit(solution)/shard_map/pack_first/pallas_call | solution.py:431
  33.0 19.0 %pack_other.1 = s32[32,248,128]{2,1,0:T(8,128)} custom-call(s32[81,128]{1,0:T(8,128)} %get-tuple-element.18.meta, s32[10368,128]{1,0:T(8,128)} %get-tuple-element.19.words), custom_call_target="tpu_custom_call" | custom-call | flops 24999999488 | bytes 21233664 | tf_op jit(solution)/shard_map/pack_other/pallas_call | solution.py:451
  51.9 98.2 %all_to_all.10.slots.words = s32[32,248,128]{2,1,0:T(8,128)} all-to-all(s32[32,248,128]{2,1,0:T(8,128)} %pack_other.1), channel_id=1, replica_groups=mesh['dp'=4,'tensor'=8] {'dp','tensor'}, dimensions={0} | all-to-all | bytes 8126464 | tf_op jit(solution)/shard_map/all_to_all | solution.py:583
  150.2 3.8 all-to-all-start
  154.0 19.8 %shard_map.85 = (bf16[72,4608]{1,0:T(8,128)(2,1)}, bf16[72,4608]{1,0:T(8,128)(2,1)}, s32[10368,128]{1,0:T(8,128)}) custom-call(s32[32,248,128]{2,1,0:T(8,128)} %all_to_all.10.slots.words, s32[32,248,128]{2,1,0:T(8,128)} %all_to_all.10.slots.words, bf16[10368,128]{1,0:T(8,128)(2,1)} %grad.5), custom_call_target="tpu_custom_call" | custom-call | flops 24999999488 | bytes 21233664 | tf_op jit(solution)/shard_map/pallas_call | solution.py:469
  174.2 70.6 %all-to-all-done.slots.words = s32[32,248,128]{2,1,0:T(8,128)} async-done(((s32[32,248,128]{2,1,0:T(8,128)}), s32[32,248,128]{2,1,0:T(8,128)}, u32[]{:S(2)}, u32[]{:S(2)}) %all-to-all-start) | async-done | bytes 4063264 | tf_op jit(solution)/shard_map/all_to_all | solution.py:583
  244.8 19.7 %shard_map.84 = (bf16[72,4608]{1,0:T(8,128)(2,1)}, bf16[72,4608]{1,0:T(8,128)(2,1)}, s32[10368,128]{1,0:T(8,128)}) custom-call(s32[32,248,128]{2,1,0:T(8,128)} %all-to-all-done.slots.words, s32[32,248,128]{2,1,0:T(8,128)} %all-to-all-done.slots.words, bf16[10368,128]{1,0:T(8,128)(2,1)} %grad.5), custom_call_target="tpu_custom_call" | custom-call | flops 24999999488 | bytes 21233664 | tf_op jit(solution)/shard_map/pallas_call | solution.py:469
  265.0 1.4 collective-permute-start.6
  266.5 1.6 collective-permute-start.9
  270.0 1.4 collective-permute-start
  274.5 8.6 %collective-permute-done.6.refs_4_ = bf16[72,4608]{1,0:T(8,128)(2,1)S(1)} collective-permute-done((bf16[72,4608]{1,0:T(8,128)(2,1)}, bf16[72,4608]{1,0:T(8,128)(2,1)S(1)}, u32[]{:S(2)}, u32[]{:S(2)}) %collective-permute-start.6) | collective-permute-done | bytes 663584 | tf_op jit(solution)/shard_map/ppermute | solution.py:555
  284.5 1.6 collective-permute-start.13
  286.0 11.2 %collective-permute-done.19.refs_5_ = bf16[72,4608]{1,0:T(8,128)(2,1)S(1)} collective-permute-done((bf16[72,4608]{1,0:T(8,128)(2,1)}, bf16[72,4608]{1,0:T(8,128)(2,1)S(1)}, u32[]{:S(2)}, u32[]{:S(2)}) %collective-permute-start.19) | collective-permute-done | bytes 663584 | tf_op jit(solution)/shard_map/ppermute | solution.py:555
  298.7 12.8 %collective-permute-done.refs_0_ = bf16[72,4608]{1,0:T(8,128)(2,1)S(1)} collective-permute-done((bf16[72,4608]{1,0:T(8,128)(2,1)}, bf16[72,4608]{1,0:T(8,128)(2,1)S(1)}, u32[]{:S(2)}, u32[]{:S(2)}) %collective-permute-start) | collective-permute-done | bytes 663584 | tf_op jit(solution)/shard_map/ppermute | solution.py:555
  311.5 16.6 %state_rows.1 = (f32[10368,128]{1,0:T(8,128)}, f32[10368,128]{1,0:T(8,128)}, f32[10368,128]{1,0:T(8,128)}) custom-call(s32[10368,128]{1,0:T(8,128)} %get-tuple-element.17.rows0, s32[10368,128]{1,0:T(8,128)} %get-tuple-element.20.rows1, bf16[10368,128]{1,0:T(8,128)(2,1)} %grad.5), custom_call_target="tpu_custom_call" | custom-call | flops 15000000512 | bytes 29196288 | tf_op jit(solution)/shard_map/state_rows/pallas_call | solution.py:504
  329.4 7.4 %shard_map.86.refs_8_ = bf16[576,18432]{1,0:T(8,128)(2,1)} custom-call(s32[4]{0:T(128)} %pad_add_fusion.4.shards, bf16[72,4608]{1,0:T(8,128)(2,1)} %get-tuple-element.24.refs_0_, bf16[72,4608]{1,0:T(8,128)(2,1)} %get-tuple-element.25.refs_1_, bf16[72,4608]{1,0:T(8,128)(2,1)} %collective-permute-done.24.refs_2_, bf16[72,4608]{1,0:T(8,128)(2,1)} %copy-done.11, ...), custom_call_target="tpu_custom_call" | custom-call | flops 8000000000 | bytes 10616832 | tf_op jit(solution)/shard_map/pallas_call | solution.py:526
  336.8 1.5 collective-permute-start.10
  338.3 1.6 collective-permute-start.7
  340.9 7.4 %shard_map.87.refs_8_ = bf16[576,18432]{1,0:T(8,128)(2,1)} custom-call(s32[4]{0:T(128)} %pad_add_fusion.3.shards, bf16[72,4608]{1,0:T(8,128)(2,1)} %copy-done.2, bf16[72,4608]{1,0:T(8,128)(2,1)} %collective-permute-done.13.refs_1_, bf16[72,4608]{1,0:T(8,128)(2,1)} %collective-permute-done.15.refs_2_, ...), custom_call_target="tpu_custom_call", output_to_operand_aliasing={{}: (9, {})} | custom-call | flops 8000000000 | bytes 10616832 | tf_op jit(solution)/shard_map/pallas_call | solution.py:526
  348.3 6.4 %collective-permute-done.10.refs_3_ = bf16[72,4608]{1,0:T(8,128)(2,1)} collective-permute-done((bf16[72,4608]{1,0:T(8,128)(2,1)S(1)}, bf16[72,4608]{1,0:T(8,128)(2,1)}, u32[]{:S(2)}, u32[]{:S(2)}) %collective-permute-start.10) | collective-permute-done | bytes 663584 | tf_op jit(solution)/shard_map/ppermute | solution.py:555
  356.1 13.3 %collective-permute-done.1.refs_0_ = bf16[72,4608]{1,0:T(8,128)(2,1)} collective-permute-done((bf16[72,4608]{1,0:T(8,128)(2,1)S(1)}, bf16[72,4608]{1,0:T(8,128)(2,1)}, u32[]{:S(2)}, u32[]{:S(2)}) %collective-permute-start.1) | collective-permute-done | bytes 663584 | tf_op jit(solution)/shard_map/ppermute | solution.py:555
  370.8 7.4 %shard_map.88.refs_4_ = bf16[576,18432]{1,0:T(8,128)(2,1)} custom-call(s32[4]{0:T(128)} %pad_add_fusion.2.shards, bf16[72,4608]{1,0:T(8,128)(2,1)} %collective-permute-done.12.refs_0_, bf16[72,4608]{1,0:T(8,128)(2,1)} %collective-permute-done.14.refs_1_, bf16[72,4608]{1,0:T(8,128)(2,1)} %copy-done.5, ...), custom_call_target="tpu_custom_call", output_to_operand_aliasing={{}: (9, {})} | custom-call | flops 8000000000 | bytes 10616832 | tf_op jit(solution)/shard_map/pallas_call | solution.py:526
  378.1 4.8 %shard_map.89.refs_4_ = bf16[576,18432]{1,0:T(8,128)(2,1)} custom-call(s32[2]{0:T(128)} %pad_add_fusion.1.shards, bf16[72,4608]{1,0:T(8,128)(2,1)} %collective-permute-done.1.refs_0_, bf16[72,4608]{1,0:T(8,128)(2,1)} %collective-permute-done.4.refs_1_, bf16[72,4608]{1,0:T(8,128)(2,1)} %copy-done.6, ...), custom_call_target="tpu_custom_call", output_to_operand_aliasing={{}: (5, {})} | custom-call | flops 4000000000 | bytes 5308416 | tf_op jit(solution)/shard_map/pallas_call | solution.py:526
  384.2 4.8 %shard_map.90 = bf16[576,18432]{1,0:T(8,128)(2,1)} custom-call(s32[2]{0:T(128)} %pad_add_fusion.shards, bf16[72,4608]{1,0:T(8,128)(2,1)} %copy-done.9, bf16[72,4608]{1,0:T(8,128)(2,1)} %collective-permute-done.5.refs_1_, bf16[72,4608]{1,0:T(8,128)(2,1)} %copy-done.8, bf16[72,4608]{1,0:T(8,128)(2,1)} %copy-done.7, ...), custom_call_target="tpu_custom_call", output_to_operand_aliasing={{}: (5, {})} | custom-call | flops 4000000000 | bytes 5308416 | tf_op jit(solution)/shard_map/pallas_call | solution.py:526
  (74 shorter events, 15.2 us)
Async XLA Ops:
  150.2 94.7 %all-to-all-start = ((s32[32,248,128]{2,1,0:T(8,128)}), s32[32,248,128]{2,1,0:T(8,128)}, u32[]{:S(2)}, u32[]{:S(2)}) async-start(s32[32,248,128]{2,1,0:T(8,128)} %get-tuple-element.16), calls=%async_computation | async-start | bytes 8126464 | tf_op jit(solution)/shard_map/all_to_all | solution.py:583
  173.7 92.8 %collective-permute-start.26 = (bf16[72,4608]{1,0:T(8,128)(2,1)}, bf16[72,4608]{1,0:T(8,128)(2,1)}, u32[]{:S(2)}, u32[]{:S(2)}) collective-permute-start(bf16[72,4608]{1,0:T(8,128)(2,1)} %get-tuple-element.26.refs_4_), channel_id=1, source_target_pairs={{0,1},{1,0},{2,3},{3,2},{4,5},{5,4},{6,7},{7,6},{8,9},{9,8},{10,11... | collective-permute-start | bytes 1990664 | tf_op jit(solution)/shard_map/ppermute | solution.py:555
  173.9 94.1 %collective-permute-start.27 = (bf16[72,4608]{1,0:T(8,128)(2,1)}, bf16[72,4608]{1,0:T(8,128)(2,1)S(1)}, u32[]{:S(2)}, u32[]{:S(2)}) collective-permute-start(bf16[72,4608]{1,0:T(8,128)(2,1)} %get-tuple-element.27.refs_5_), channel_id=1, source_target_pairs={{0,1},{1,0},{2,3},{3,2},{4,5},{5,4},{6,7},{7,6},{8,9},{9,8},{10,11... | collective-permute-start | bytes 1990664 | tf_op jit(solution)/shard_map/ppermute | solution.py:555
  265.0 18.0 %collective-permute-start.6 = (bf16[72,4608]{1,0:T(8,128)(2,1)}, bf16[72,4608]{1,0:T(8,128)(2,1)S(1)}, u32[]{:S(2)}, u32[]{:S(2)}) collective-permute-start(bf16[72,4608]{1,0:T(8,128)(2,1)} %get-tuple-element.26.refs_4_), channel_id=1, source_target_pairs={{0,2},{1,3},{2,0},{3,1},{4,6},{5,7},{6,4},{7,5},{8,10},{9,11},{10,... | collective-permute-start | bytes 1990664 | tf_op jit(solution)/shard_map/ppermute | solution.py:555
  266.5 18.0 %collective-permute-start.9 = (bf16[72,4608]{1,0:T(8,128)(2,1)}, bf16[72,4608]{1,0:T(8,128)(2,1)S(1)}, u32[]{:S(2)}, u32[]{:S(2)}) collective-permute-start(bf16[72,4608]{1,0:T(8,128)(2,1)} %get-tuple-element.27.refs_5_), channel_id=1, source_target_pairs={{0,4},{1,5},{2,6},{3,7},{4,0},{5,1},{6,2},{7,3},{8,12},{9,13},{10,... | collective-permute-start | bytes 1990664 | tf_op jit(solution)/shard_map/ppermute | solution.py:555
  268.1 29.2 %collective-permute-start.19 = (bf16[72,4608]{1,0:T(8,128)(2,1)}, bf16[72,4608]{1,0:T(8,128)(2,1)S(1)}, u32[]{:S(2)}, u32[]{:S(2)}) collective-permute-start(bf16[72,4608]{1,0:T(8,128)(2,1)} %get-tuple-element.27.refs_5_), channel_id=1, source_target_pairs={{0,2},{1,3},{2,0},{3,1},{4,6},{5,7},{6,4},{7,5},{8,10},{9,11},{10,... | collective-permute-start | bytes 1990664 | tf_op jit(solution)/shard_map/ppermute | solution.py:555
  268.5 30.2 %collective-permute-start.21 = (bf16[72,4608]{1,0:T(8,128)(2,1)}, bf16[72,4608]{1,0:T(8,128)(2,1)S(1)}, u32[]{:S(2)}, u32[]{:S(2)}) collective-permute-start(bf16[72,4608]{1,0:T(8,128)(2,1)} %get-tuple-element.26.refs_4_), channel_id=1, source_target_pairs={{0,4},{1,5},{2,6},{3,7},{4,0},{5,1},{6,2},{7,3},{8,12},{9,13},{10,... | collective-permute-start | bytes 1990664 | tf_op jit(solution)/shard_map/ppermute | solution.py:555
  270.0 41.4 %collective-permute-start = (bf16[72,4608]{1,0:T(8,128)(2,1)}, bf16[72,4608]{1,0:T(8,128)(2,1)S(1)}, u32[]{:S(2)}, u32[]{:S(2)}) collective-permute-start(bf16[72,4608]{1,0:T(8,128)(2,1)} %get-tuple-element.24.refs_0_), channel_id=1, source_target_pairs={{0,2},{1,3},{2,0},{3,1},{4,6},{5,7},{6,4},{7,5},{8,10},{9,11},{10,... | collective-permute-start | bytes 1990664 | tf_op jit(solution)/shard_map/ppermute | solution.py:555
  283.0 45.0 %collective-permute-start.3 = (bf16[72,4608]{1,0:T(8,128)(2,1)}, bf16[72,4608]{1,0:T(8,128)(2,1)}, u32[]{:S(2)}, u32[]{:S(2)}) collective-permute-start(bf16[72,4608]{1,0:T(8,128)(2,1)} %get-tuple-element.25.refs_1_), channel_id=1, source_target_pairs={{0,4},{1,5},{2,6},{3,7},{4,0},{5,1},{6,2},{7,3},{8,12},{9,13},{10,... | collective-permute-start | bytes 1990664 | tf_op jit(solution)/shard_map/ppermute | solution.py:555
  284.5 43.9 %collective-permute-start.13 = (bf16[72,4608]{1,0:T(8,128)(2,1)}, bf16[72,4608]{1,0:T(8,128)(2,1)}, u32[]{:S(2)}, u32[]{:S(2)}) collective-permute-start(bf16[72,4608]{1,0:T(8,128)(2,1)} %get-tuple-element.25.refs_1_), channel_id=1, source_target_pairs={{0,2},{1,3},{2,0},{3,1},{4,6},{5,7},{6,4},{7,5},{8,10},{9,11},{10,... | collective-permute-start | bytes 1990664 | tf_op jit(solution)/shard_map/ppermute | solution.py:555
  297.3 31.4 %collective-permute-start.15 = (bf16[72,4608]{1,0:T(8,128)(2,1)}, bf16[72,4608]{1,0:T(8,128)(2,1)}, u32[]{:S(2)}, u32[]{:S(2)}) collective-permute-start(bf16[72,4608]{1,0:T(8,128)(2,1)} %get-tuple-element.24.refs_0_), channel_id=1, source_target_pairs={{0,4},{1,5},{2,6},{3,7},{4,0},{5,1},{6,2},{7,3},{8,12},{9,13},{10,... | collective-permute-start | bytes 1990664 | tf_op jit(solution)/shard_map/ppermute | solution.py:555
  298.7 30.2 %collective-permute-start.18 = (bf16[72,4608]{1,0:T(8,128)(2,1)S(1)}, bf16[72,4608]{1,0:T(8,128)(2,1)}, u32[]{:S(2)}, u32[]{:S(2)}) collective-permute-start(bf16[72,4608]{1,0:T(8,128)(2,1)S(1)} %collective-permute-done.6.refs_4_), channel_id=1, source_target_pairs={{0,1},{1,0},{2,3},{3,2},{4,5},{5,4},{6,7},{7,6},{8,9},{9,8},{10,11... | collective-permute-start | bytes 1990664 | tf_op jit(solution)/shard_map/ppermute | solution.py:555
  311.5 17.7 %collective-permute-start.23 = (bf16[72,4608]{1,0:T(8,128)(2,1)S(1)}, bf16[72,4608]{1,0:T(8,128)(2,1)}, u32[]{:S(2)}, u32[]{:S(2)}) collective-permute-start(bf16[72,4608]{1,0:T(8,128)(2,1)S(1)} %collective-permute-done.9.refs_7_), channel_id=1, source_target_pairs={{0,1},{1,0},{2,3},{3,2},{4,5},{5,4},{6,7},{7,6},{8,9},{9,8},{10,11... | collective-permute-start | bytes 1990664 | tf_op jit(solution)/shard_map/ppermute | solution.py:555
  328.9 11.4 %collective-permute-start.17 = (bf16[72,4608]{1,0:T(8,128)(2,1)}, bf16[72,4608]{1,0:T(8,128)(2,1)}, u32[]{:S(2)}, u32[]{:S(2)}) collective-permute-start(bf16[72,4608]{1,0:T(8,128)(2,1)} %collective-permute-done.3.refs_3_), channel_id=1, source_target_pairs={{0,1},{1,0},{2,3},{3,2},{4,5},{5,4},{6,7},{7,6},{8,9},{9,8},{10,11... | collective-permute-start | bytes 1990664 | tf_op jit(solution)/shard_map/ppermute | solution.py:555
  329.2 11.8 %collective-permute-start.14 = (bf16[72,4608]{1,0:T(8,128)(2,1)}, bf16[72,4608]{1,0:T(8,128)(2,1)}, u32[]{:S(2)}, u32[]{:S(2)}) collective-permute-start(bf16[72,4608]{1,0:T(8,128)(2,1)} %collective-permute-done.13.refs_1_), channel_id=1, source_target_pairs={{0,1},{1,0},{2,3},{3,2},{4,5},{5,4},{6,7},{7,6},{8,9},{9,8},{10,11... | collective-permute-start | bytes 1990664 | tf_op jit(solution)/shard_map/ppermute | solution.py:555
  336.8 18.0 %collective-permute-start.10 = (bf16[72,4608]{1,0:T(8,128)(2,1)S(1)}, bf16[72,4608]{1,0:T(8,128)(2,1)}, u32[]{:S(2)}, u32[]{:S(2)}) collective-permute-start(bf16[72,4608]{1,0:T(8,128)(2,1)S(1)} %collective-permute-done.9.refs_7_), channel_id=1, source_target_pairs={{0,2},{1,3},{2,0},{3,1},{4,6},{5,7},{6,4},{7,5},{8,10},{9,11},{10,... | collective-permute-start | bytes 1990664 | tf_op jit(solution)/shard_map/ppermute | solution.py:555
  338.3 17.8 %collective-permute-start.7 = (bf16[72,4608]{1,0:T(8,128)(2,1)S(1)}, bf16[72,4608]{1,0:T(8,128)(2,1)S(1)}, u32[]{:S(2)}, u32[]{:S(2)}) collective-permute-start(bf16[72,4608]{1,0:T(8,128)(2,1)S(1)} %collective-permute-done.6.refs_4_), channel_id=1, source_target_pairs={{0,4},{1,5},{2,6},{3,7},{4,0},{5,1},{6,2},{7,3},{8,12},{9,13},{10,... | collective-permute-start | bytes 1990664 | tf_op jit(solution)/shard_map/ppermute | solution.py:555
  339.9 29.5 %collective-permute-start.1 = (bf16[72,4608]{1,0:T(8,128)(2,1)S(1)}, bf16[72,4608]{1,0:T(8,128)(2,1)}, u32[]{:S(2)}, u32[]{:S(2)}) collective-permute-start(bf16[72,4608]{1,0:T(8,128)(2,1)S(1)} %collective-permute-done.refs_0_), channel_id=1, source_target_pairs={{0,4},{1,5},{2,6},{3,7},{4,0},{5,1},{6,2},{7,3},{8,12},{9,13},{10,... | collective-permute-start | bytes 1990664 | tf_op jit(solution)/shard_map/ppermute | solution.py:555
  340.3 29.1 %collective-permute-start.4 = (bf16[72,4608]{1,0:T(8,128)(2,1)}, bf16[72,4608]{1,0:T(8,128)(2,1)}, u32[]{:S(2)}, u32[]{:S(2)}) collective-permute-start(bf16[72,4608]{1,0:T(8,128)(2,1)} %collective-permute-done.3.refs_3_), channel_id=1, source_target_pairs={{0,2},{1,3},{2,0},{3,1},{4,6},{5,7},{6,4},{7,5},{8,10},{9,11},{10,... | collective-permute-start | bytes 1990664 | tf_op jit(solution)/shard_map/ppermute | solution.py:555
  340.9 29.0 %collective-permute-start.16 = (bf16[72,4608]{1,0:T(8,128)(2,1)}, bf16[72,4608]{1,0:T(8,128)(2,1)S(1)}, u32[]{:S(2)}, u32[]{:S(2)}) collective-permute-start(bf16[72,4608]{1,0:T(8,128)(2,1)} %collective-permute-done.15.refs_2_), channel_id=1, source_target_pairs={{0,1},{1,0},{2,3},{3,2},{4,5},{5,4},{6,7},{7,6},{8,9},{9,8},{10,11... | collective-permute-start | bytes 1990664 | tf_op jit(solution)/shard_map/ppermute | solution.py:555
  354.7 28.2 %collective-permute-start.11 = (bf16[72,4608]{1,0:T(8,128)(2,1)}, bf16[72,4608]{1,0:T(8,128)(2,1)S(1)}, u32[]{:S(2)}, u32[]{:S(2)}) collective-permute-start(bf16[72,4608]{1,0:T(8,128)(2,1)} %collective-permute-done.10.refs_3_), channel_id=1, source_target_pairs={{0,1},{1,0},{2,3},{3,2},{4,5},{5,4},{6,7},{7,6},{8,9},{9,8},{10,11... | collective-permute-start | bytes 1990664 | tf_op jit(solution)/shard_map/ppermute | solution.py:555
  356.1 26.9 %collective-permute-start.8 = (bf16[72,4608]{1,0:T(8,128)(2,1)S(1)}, bf16[72,4608]{1,0:T(8,128)(2,1)S(1)}, u32[]{:S(2)}, u32[]{:S(2)}) collective-permute-start(bf16[72,4608]{1,0:T(8,128)(2,1)S(1)} %collective-permute-done.7.refs_2_), channel_id=1, source_target_pairs={{0,1},{1,0},{2,3},{3,2},{4,5},{5,4},{6,7},{7,6},{8,9},{9,8},{10,11... | collective-permute-start | bytes 1990664 | tf_op jit(solution)/shard_map/ppermute | solution.py:555
  369.4 13.6 %collective-permute-start.2 = (bf16[72,4608]{1,0:T(8,128)(2,1)}, bf16[72,4608]{1,0:T(8,128)(2,1)S(1)}, u32[]{:S(2)}, u32[]{:S(2)}) collective-permute-start(bf16[72,4608]{1,0:T(8,128)(2,1)} %collective-permute-done.1.refs_0_), channel_id=1, source_target_pairs={{0,1},{1,0},{2,3},{3,2},{4,5},{5,4},{6,7},{7,6},{8,9},{9,8},{10,11... | collective-permute-start | bytes 1990664 | tf_op jit(solution)/shard_map/ppermute | solution.py:555
  369.4 13.6 %collective-permute-start.5 = (bf16[72,4608]{1,0:T(8,128)(2,1)}, bf16[72,4608]{1,0:T(8,128)(2,1)}, u32[]{:S(2)}, u32[]{:S(2)}) collective-permute-start(bf16[72,4608]{1,0:T(8,128)(2,1)} %collective-permute-done.4.refs_1_), channel_id=1, source_target_pairs={{0,1},{1,0},{2,3},{3,2},{4,5},{5,4},{6,7},{7,6},{8,9},{9,8},{10,11... | collective-permute-start | bytes 1990664 | tf_op jit(solution)/shard_map/ppermute | solution.py:555
  (17 other events, 263.0 us)

commit v6 on v5

--- a/solution.py
+++ b/solution.py
@@ -87,7 +87,7 @@
         self.slot_tile = self.slot_at // 8
         self.seg = math.gcd(rows, LANES)
         self.lines = rows // self.seg
-        self.tiles = next(n for n in (3, 2, 4, 1) if self.lines % n == 0)
+        self.tiles = next(n for n in (9, 3, 2, 4, 1) if self.lines % n == 0)
         self.tile_rows = rows // self.tiles
         self.tile_lines = self.lines // self.tiles
         self.dests = next(n for n in (8, 4, 2, 1) if devices % n == 0)
@@ -127,7 +127,7 @@
         return rank
 
     rank = lax.fori_loop(0, (sz.devices + 7) // 8, body, jnp.zeros((n, seg), jnp.float32))
-    return (slot << 16) | (target * sz.stride + rank.astype(jnp.int32))
+    return slot, target * sz.stride + rank.astype(jnp.int32)
 
 
 def fill_rows(sz, rows):
@@ -139,7 +139,12 @@
     lax.fori_loop(0, sz.devices, fill, 0)
 
 
-def encode_lines(sz, states, i, first_half, other_half):
+def encode_lines(sz, states, slots, line, i, first_half, other_half):
+    slot = slots[pl.ds(line + i, 1), :].astype(jnp.float32)
+    square = (sz.seg, sz.seg)
+    row = lax.broadcasted_iota(jnp.int32, square, 0)
+    slot = jnp.sum(jnp.where(row == lane_of(square), slot, 0.0), axis=1, keepdims=True)
+    slot = slot.astype(jnp.int32) << 16
     at = pl.ds(pl.multiple_of(i * sz.seg, 8), sz.seg)
     master, moment, second = (state[at, :] for state in states)
     code_m = log_code(master, MASTER_INV, MASTER_STEPS)
@@ -150,20 +155,18 @@
     lane = lane_of(word.shape)
     used = lane < HALF + QUARTER
     first_half[...] = jnp.where(
-        lane < HALF, word, jnp.where(used, pltpu.roll(pair, HALF, 1), 0)
+        lane < HALF, word, jnp.where(used, pltpu.roll(pair, HALF, 1), slot)
     )
     other_half[at, :] = jnp.where(
-        lane < HALF, pltpu.roll(word, HALF, 1), jnp.where(used, pair, 0)
+        lane < HALF, pltpu.roll(word, HALF, 1), jnp.where(used, pair, slot)
     )
 
 
 def scatter_line(sz, meta, line, words, base, rows):
-    free = lane_of((1, LANES)) >= HALF + QUARTER
     for at in range(0, sz.seg, 8):
         values = [words[pl.ds(base + at + u, 1), :] for u in range(8)]
         for u in range(8):
-            m = meta[line, at + u]
-            rows[pl.ds(m & 0xFFFF, 1), :] = jnp.where(free, m, values[u])
+            rows[pl.ds(meta[line, at + u], 1), :] = values[u]
 
 
 def pack_piece(sz, rows, base, out, dd):
@@ -218,13 +221,13 @@
 
 
 def pack_first_kernel(
-    sz, block, master, moment, second, out, other, meta_out, rows, meta, meta_vec, even, odd, sem
+    sz, block, master, moment, second, out, other, meta_out, rows, meta, meta_vec, slots, even, odd, sem
 ):
     step = pl.program_id(0)
 
     @pl.when(step == 0)
     def _():
-        meta_vec[...] = bucket_index(sz, block[...])
+        slots[...], meta_vec[...] = bucket_index(sz, block[...])
         copies = [
             pltpu.make_async_copy(meta_vec, meta, sem.at[0]),
             pltpu.make_async_copy(meta_vec, meta_out, sem.at[1]),
@@ -239,14 +242,15 @@
     def _():
         states = (master, moment, second)
         n = sz.tile_lines
-        encode_lines(sz, states, 0, even, other)
+        first = step * n
+        encode_lines(sz, states, slots, first, 0, even, other)
 
         def body(i, carry):
             line = step * n + 2 * i
             scatter_line(sz, meta, line, even, 0, rows)
-            encode_lines(sz, states, 2 * i + 1, odd, other)
+            encode_lines(sz, states, slots, first, 2 * i + 1, odd, other)
             scatter_line(sz, meta, line + 1, odd, 0, rows)
-            encode_lines(sz, states, jnp.minimum(2 * i + 2, n - 1), even, other)
+            encode_lines(sz, states, slots, first, jnp.minimum(2 * i + 2, n - 1), even, other)
             return carry
 
         lax.fori_loop(0, n // 2, body, 0)
@@ -393,7 +397,7 @@
 
 def join_tile(first, other, weight):
     blocks = first.shape[1] // LANES
-    unroll = next(n for n in (12, 9, 8, 6, 4, 3, 2, 1) if blocks % n == 0)
+    unroll = next(n for n in (36, 12, 9, 8, 6, 4, 3, 2, 1) if blocks % n == 0)
     low = lane_of((first.shape[0], LANES)) < HALF
 
     def body(i, carry):
@@ -441,6 +445,7 @@
         scratch_shapes=[
             places,
             pltpu.SMEM(lines, jnp.int32),
+            pltpu.VMEM(lines, jnp.int32),
             pltpu.VMEM(lines, jnp.int32),
             pltpu.VMEM((sz.seg, LANES), jnp.int32),
             pltpu.VMEM((sz.seg, LANES), jnp.int32),
@@ -512,14 +517,13 @@
     )(rows0, rows1, gradient)
 
 
-def join_call(sz, keys, firsts, others, weight):
-    me = lax.axis_index("tensor")
+def join_call(sz, shards, keys, firsts, others, weight):
     count = len(keys)
-    where = jnp.stack([me ^ mask for mask, _ in keys]).astype(jnp.int32)
     parts = [part for _, part in keys]
 
     def place(i, shards):
-        return shards[i], sum(jnp.where(i == q, p, 0) for q, p in enumerate(parts))
+        mask = sum(jnp.where(i == q, k, 0) for q, (k, _) in enumerate(keys))
+        return shards[mask], sum(jnp.where(i == q, p, 0) for q, p in enumerate(parts))
 
     tiles = [pl.BlockSpec((sz.w_rows, FF_WIN // 4), lambda i, shards: (0, 0))] * count
     again = [] if weight is None else [weight]
@@ -534,7 +538,7 @@
         out_shape=jax.ShapeDtypeStruct((sz.w_rows * sz.n_tensor, FF_WIN), jnp.bfloat16),
         input_output_aliases={1 + 2 * count: 0} if again else {},
         cost_estimate=cost(2 * count, 8 * count * sz.w_rows * FF_WIN // 4),
-    )(where, *firsts, *others, *again)
+    )(shards, *firsts, *others, *again)
 
 
 def whole_join_call(sz, first, other):
@@ -593,6 +597,7 @@
     if not by_hops:
         return (*outs, whole_join_call(sz, *halves))
     weight = None
+    shards = lax.axis_index("tensor").astype(jnp.int32) ^ lax.iota(jnp.int32, n_tensor)
     masks = range(0, n_tensor, 2)
     near = [m for m in masks if m & (m - 1) == 0]
     far = [m for m in masks if m & (m - 1)]
@@ -600,7 +605,7 @@
     for group in groups:
         keys = [(mask, part) for mask in group for part in range(2)]
         firsts, others = ([half[key] for key in keys] for half in halves)
-        weight = join_call(sz, keys, firsts, others, weight)
+        weight = join_call(sz, shards, keys, firsts, others, weight)
     return (*outs, weight)
 
 

time: 390 us -> 385 us (0.987)
  Pallas kernels: 139 us -> 133 us
  waiting for transfers between devices: 124 us -> 128 us
  transfers between devices with their start and end apart: 29 -> 29, of which waited for: 7 -> 8; matrix products, arithmetic and copies ran while one was open for 1% -> 0% of each run, Pallas kernels for 21% -> 21%
where the time goes in v6:
time: 385 us; the launch traced here: 384 us
  Pallas kernels  133 us (35%)
  waiting for transfers between devices  128 us (33%)
  blocking collectives  98.2 us (26%)
  starting transfers between devices  20.8 us (5%)
    all_to_all x1, blocking collectives, per_device(): lax.all_to_all(sent[half], ('dp', 'tensor'), split_axis=0, concat_axis=0,...  98.2 us
    all_to_all x1, waiting for transfers between devices, per_device(): lax.all_to_all(sent[half], ('dp', 'tensor'), split_axis=0, concat_axis=0,...  70.6 us
    ppermute x28, waiting for transfers between devices, hop(): return lax.ppermute(value, 'tensor', pairs)  57.2 us
    pallas_call x2, Pallas kernels, place_call(): pl.pallas_call(functools.partial(place_kernel, sz, half), grid=(sources +...  39.5 us
    pallas_call x1, Pallas kernels, pack_calls(): pl.pallas_call(functools.partial(pack_first_kernel, sz), grid=grid, in_sp...  31 us
    pallas_call x5, Pallas kernels, join_call(): pl.pallas_call(functools.partial(join_kernel, count), grid_spec=pltpu.Pre...  29.3 us
    ppermute x28, starting transfers between devices, hop(): return lax.ppermute(value, 'tensor', pairs)  17.1 us
    pallas_call x1, Pallas kernels, pack_calls(): pl.pallas_call(functools.partial(pack_other_kernel, sz), grid=grid, in_sp...  16.8 us
  transfers between devices with their start and end apart: 29, of which 8 were waited for; matrix products, arithmetic and copies ran while one was open for 0% of the time, Pallas kernels for 21%

profile of v6, /device:TPU:0, one launch (start us, length us, event | category | flops | bytes accessed | tf_op | source)
XLA Modules:
  0.0 384.4 jit_solution(15204846246728066592)
XLA Ops:
  0.6 31.0 %pack_first.1 = (s32[32,248,128]{2,1,0:T(8,128)}, s32[10368,128]{1,0:T(8,128)}, s32[81,128]{1,0:T(8,128)}) custom-call(s32[81,128]{1,0:T(8,128)} %bitcast.1, f32[10368,128]{1,0:T(8,128)} %master.1, f32[10368,128]{1,0:T(8,128)} %moment.1, f32[10368,128]{1,0:T(8,128)} %second.1), custom_call_target="tpu_custom_call" | custom-call | tf_op jit(solution)/shard_map/pack_first/pallas_call | solution.py:435
  31.7 16.8 %pack_other.1 = s32[32,248,128]{2,1,0:T(8,128)} custom-call(s32[81,128]{1,0:T(8,128)} %get-tuple-element.18.meta, s32[10368,128]{1,0:T(8,128)} %get-tuple-element.19.words), custom_call_target="tpu_custom_call" | custom-call | flops 24999999488 | bytes 21233664 | tf_op jit(solution)/shard_map/pack_other/pallas_call | solution.py:456
  48.4 98.2 %all_to_all.10.slots.words = s32[32,248,128]{2,1,0:T(8,128)} all-to-all(s32[32,248,128]{2,1,0:T(8,128)} %pack_other.1), channel_id=1, replica_groups=mesh['dp'=4,'tensor'=8] {'dp','tensor'}, dimensions={0} | all-to-all | bytes 8126464 | tf_op jit(solution)/shard_map/all_to_all | solution.py:587
  146.7 3.8 all-to-all-start
  150.5 19.8 %shard_map.85 = (bf16[72,4608]{1,0:T(8,128)(2,1)}, bf16[72,4608]{1,0:T(8,128)(2,1)}, s32[10368,128]{1,0:T(8,128)}) custom-call(s32[32,248,128]{2,1,0:T(8,128)} %all_to_all.10.slots.words, s32[32,248,128]{2,1,0:T(8,128)} %all_to_all.10.slots.words, bf16[10368,128]{1,0:T(8,128)(2,1)} %grad.5), custom_call_target="tpu_custom_call" | custom-call | flops 24999999488 | bytes 21233664 | tf_op jit(solution)/shard_map/pallas_call | solution.py:474
  170.7 70.6 %all-to-all-done.slots.words = s32[32,248,128]{2,1,0:T(8,128)} async-done(((s32[32,248,128]{2,1,0:T(8,128)}), s32[32,248,128]{2,1,0:T(8,128)}, u32[]{:S(2)}, u32[]{:S(2)}) %all-to-all-start) | async-done | bytes 4063264 | tf_op jit(solution)/shard_map/all_to_all | solution.py:587
  241.4 19.7 %shard_map.84 = (bf16[72,4608]{1,0:T(8,128)(2,1)}, bf16[72,4608]{1,0:T(8,128)(2,1)}, s32[10368,128]{1,0:T(8,128)}) custom-call(s32[32,248,128]{2,1,0:T(8,128)} %all-to-all-done.slots.words, s32[32,248,128]{2,1,0:T(8,128)} %all-to-all-done.slots.words, bf16[10368,128]{1,0:T(8,128)(2,1)} %grad.5), custom_call_target="tpu_custom_call" | custom-call | flops 24999999488 | bytes 21233664 | tf_op jit(solution)/shard_map/pallas_call | solution.py:474
  263.0 1.6 collective-permute-start.9
  265.9 1.6 collective-permute-start
  267.9 11.6 %collective-permute-done.6.refs_4_ = bf16[72,4608]{1,0:T(8,128)(2,1)S(1)} collective-permute-done((bf16[72,4608]{1,0:T(8,128)(2,1)}, bf16[72,4608]{1,0:T(8,128)(2,1)S(1)}, u32[]{:S(2)}, u32[]{:S(2)}) %collective-permute-start.6) | collective-permute-done | bytes 663584 | tf_op jit(solution)/shard_map/ppermute | solution.py:559
  281.0 1.6 collective-permute-start.13
  282.6 11.2 %collective-permute-done.19.refs_5_ = bf16[72,4608]{1,0:T(8,128)(2,1)S(1)} collective-permute-done((bf16[72,4608]{1,0:T(8,128)(2,1)}, bf16[72,4608]{1,0:T(8,128)(2,1)S(1)}, u32[]{:S(2)}, u32[]{:S(2)}) %collective-permute-start.19) | collective-permute-done | bytes 663584 | tf_op jit(solution)/shard_map/ppermute | solution.py:559
  295.3 12.7 %collective-permute-done.refs_0_ = bf16[72,4608]{1,0:T(8,128)(2,1)S(1)} collective-permute-done((bf16[72,4608]{1,0:T(8,128)(2,1)}, bf16[72,4608]{1,0:T(8,128)(2,1)S(1)}, u32[]{:S(2)}, u32[]{:S(2)}) %collective-permute-start) | collective-permute-done | bytes 663584 | tf_op jit(solution)/shard_map/ppermute | solution.py:559
  308.0 16.6 %state_rows.1 = (f32[10368,128]{1,0:T(8,128)}, f32[10368,128]{1,0:T(8,128)}, f32[10368,128]{1,0:T(8,128)}) custom-call(s32[10368,128]{1,0:T(8,128)} %get-tuple-element.17.rows0, s32[10368,128]{1,0:T(8,128)} %get-tuple-element.20.rows1, bf16[10368,128]{1,0:T(8,128)(2,1)} %grad.5), custom_call_target="tpu_custom_call" | custom-call | flops 15000000512 | bytes 29196288 | tf_op jit(solution)/shard_map/state_rows/pallas_call | solution.py:509
  325.9 6.8 %shard_map.86.refs_8_ = bf16[576,18432]{1,0:T(8,128)(2,1)} custom-call(s32[8]{0:T(128)} %iota_xor_fusion.shards, bf16[72,4608]{1,0:T(8,128)(2,1)} %get-tuple-element.24.refs_0_, bf16[72,4608]{1,0:T(8,128)(2,1)} %get-tuple-element.25.refs_1_, bf16[72,4608]{1,0:T(8,128)(2,1)} %copy-done.11, bf16[72,4608]{1,0:T(8,128)(2,1)} %copy-done.12, ...), custom_call_target="tpu_custom_call" | custom-call | flops 8000000000 | bytes 10616832 | tf_op jit(solution)/shard_map/pallas_call | solution.py:530
  332.7 1.5 collective-permute-start.10
  334.2 1.6 collective-permute-start.7
  336.8 7.0 %shard_map.87.refs_8_ = bf16[576,18432]{1,0:T(8,128)(2,1)} custom-call(s32[8]{0:T(128)} %iota_xor_fusion.shards, bf16[72,4608]{1,0:T(8,128)(2,1)} %copy-done.2, bf16[72,4608]{1,0:T(8,128)(2,1)} %collective-permute-done.13.refs_1_, bf16[72,4608]{1,0:T(8,128)(2,1)} %collective-permute-done.15.refs_2_, ...), custom_call_target="tpu_custom_call", output_to_operand_aliasing={{}: (9, {})} | custom-call | flops 8000000000 | bytes 10616832 | tf_op jit(solution)/shard_map/pallas_call | solution.py:530
  343.8 6.8 %collective-permute-done.10.refs_3_ = bf16[72,4608]{1,0:T(8,128)(2,1)} collective-permute-done((bf16[72,4608]{1,0:T(8,128)(2,1)S(1)}, bf16[72,4608]{1,0:T(8,128)(2,1)}, u32[]{:S(2)}, u32[]{:S(2)}) %collective-permute-start.10) | collective-permute-done | bytes 663584 | tf_op jit(solution)/shard_map/ppermute | solution.py:559
  350.7 1.4 collective-permute-done.7.refs_2_
  352.1 13.2 %collective-permute-done.1.refs_0_ = bf16[72,4608]{1,0:T(8,128)(2,1)} collective-permute-done((bf16[72,4608]{1,0:T(8,128)(2,1)S(1)}, bf16[72,4608]{1,0:T(8,128)(2,1)}, u32[]{:S(2)}, u32[]{:S(2)}) %collective-permute-start.1) | collective-permute-done | bytes 663584 | tf_op jit(solution)/shard_map/ppermute | solution.py:559
  366.7 6.8 %shard_map.88.refs_4_ = bf16[576,18432]{1,0:T(8,128)(2,1)} custom-call(s32[8]{0:T(128)} %iota_xor_fusion.shards, bf16[72,4608]{1,0:T(8,128)(2,1)} %collective-permute-done.12.refs_0_, bf16[72,4608]{1,0:T(8,128)(2,1)} %collective-permute-done.14.refs_1_, bf16[72,4608]{1,0:T(8,128)(2,1)} %copy-done.5, ...), custom_call_target="tpu_custom_call", output_to_operand_aliasing={{}: (9, {})} | custom-call | flops 8000000000 | bytes 10616832 | tf_op jit(solution)/shard_map/pallas_call | solution.py:530
  373.5 4.4 %shard_map.89.refs_4_ = bf16[576,18432]{1,0:T(8,128)(2,1)} custom-call(s32[8]{0:T(128)} %iota_xor_fusion.shards, bf16[72,4608]{1,0:T(8,128)(2,1)} %collective-permute-done.1.refs_0_, bf16[72,4608]{1,0:T(8,128)(2,1)} %collective-permute-done.4.refs_1_, bf16[72,4608]{1,0:T(8,128)(2,1)} %collective-permute-done.7.refs_2_, ...), custom_call_target="tpu_custom_call", output_to_operand_aliasing={{}: (5, {})} | custom-call | flops 4000000000 | bytes 5308416 | tf_op jit(solution)/shard_map/pallas_call | solution.py:530
  380.0 4.4 %shard_map.90 = bf16[576,18432]{1,0:T(8,128)(2,1)} custom-call(s32[8]{0:T(128)} %iota_xor_fusion.shards, bf16[72,4608]{1,0:T(8,128)(2,1)} %copy-done.8, bf16[72,4608]{1,0:T(8,128)(2,1)} %copy-done.9, bf16[72,4608]{1,0:T(8,128)(2,1)} %copy-done.7, bf16[72,4608]{1,0:T(8,128)(2,1)} %copy-done.6, ...), custom_call_target="tpu_custom_call", output_to_operand_aliasing={{}: (5, {})} | custom-call | flops 4000000000 | bytes 5308416 | tf_op jit(solution)/shard_map/pallas_call | solution.py:530
  (72 shorter events, 13.2 us)
Async XLA Ops:
  146.7 94.7 %all-to-all-start = ((s32[32,248,128]{2,1,0:T(8,128)}), s32[32,248,128]{2,1,0:T(8,128)}, u32[]{:S(2)}, u32[]{:S(2)}) async-start(s32[32,248,128]{2,1,0:T(8,128)} %get-tuple-element.16), calls=%async_computation | async-start | bytes 8126464 | tf_op jit(solution)/shard_map/all_to_all | solution.py:587
  170.2 92.8 %collective-permute-start.26 = (bf16[72,4608]{1,0:T(8,128)(2,1)}, bf16[72,4608]{1,0:T(8,128)(2,1)}, u32[]{:S(2)}, u32[]{:S(2)}) collective-permute-start(bf16[72,4608]{1,0:T(8,128)(2,1)} %get-tuple-element.26.refs_4_), channel_id=1, source_target_pairs={{0,1},{1,0},{2,3},{3,2},{4,5},{5,4},{6,7},{7,6},{8,9},{9,8},{10,11... | collective-permute-start | bytes 1990664 | tf_op jit(solution)/shard_map/ppermute | solution.py:559
  170.4 94.2 %collective-permute-start.27 = (bf16[72,4608]{1,0:T(8,128)(2,1)}, bf16[72,4608]{1,0:T(8,128)(2,1)S(1)}, u32[]{:S(2)}, u32[]{:S(2)}) collective-permute-start(bf16[72,4608]{1,0:T(8,128)(2,1)} %get-tuple-element.27.refs_5_), channel_id=1, source_target_pairs={{0,1},{1,0},{2,3},{3,2},{4,5},{5,4},{6,7},{7,6},{8,9},{9,8},{10,11... | collective-permute-start | bytes 1990664 | tf_op jit(solution)/shard_map/ppermute | solution.py:559
  261.6 18.0 %collective-permute-start.6 = (bf16[72,4608]{1,0:T(8,128)(2,1)}, bf16[72,4608]{1,0:T(8,128)(2,1)S(1)}, u32[]{:S(2)}, u32[]{:S(2)}) collective-permute-start(bf16[72,4608]{1,0:T(8,128)(2,1)} %get-tuple-element.26.refs_4_), channel_id=1, source_target_pairs={{0,2},{1,3},{2,0},{3,1},{4,6},{5,7},{6,4},{7,5},{8,10},{9,11},{10,... | collective-permute-start | bytes 1990664 | tf_op jit(solution)/shard_map/ppermute | solution.py:559
  263.0 18.0 %collective-permute-start.9 = (bf16[72,4608]{1,0:T(8,128)(2,1)}, bf16[72,4608]{1,0:T(8,128)(2,1)S(1)}, u32[]{:S(2)}, u32[]{:S(2)}) collective-permute-start(bf16[72,4608]{1,0:T(8,128)(2,1)} %get-tuple-element.27.refs_5_), channel_id=1, source_target_pairs={{0,4},{1,5},{2,6},{3,7},{4,0},{5,1},{6,2},{7,3},{8,12},{9,13},{10,... | collective-permute-start | bytes 1990664 | tf_op jit(solution)/shard_map/ppermute | solution.py:559
  264.6 29.2 %collective-permute-start.19 = (bf16[72,4608]{1,0:T(8,128)(2,1)}, bf16[72,4608]{1,0:T(8,128)(2,1)S(1)}, u32[]{:S(2)}, u32[]{:S(2)}) collective-permute-start(bf16[72,4608]{1,0:T(8,128)(2,1)} %get-tuple-element.27.refs_5_), channel_id=1, source_target_pairs={{0,2},{1,3},{2,0},{3,1},{4,6},{5,7},{6,4},{7,5},{8,10},{9,11},{10,... | collective-permute-start | bytes 1990664 | tf_op jit(solution)/shard_map/ppermute | solution.py:559
  265.0 30.3 %collective-permute-start.21 = (bf16[72,4608]{1,0:T(8,128)(2,1)}, bf16[72,4608]{1,0:T(8,128)(2,1)}, u32[]{:S(2)}, u32[]{:S(2)}) collective-permute-start(bf16[72,4608]{1,0:T(8,128)(2,1)} %get-tuple-element.26.refs_4_), channel_id=1, source_target_pairs={{0,4},{1,5},{2,6},{3,7},{4,0},{5,1},{6,2},{7,3},{8,12},{9,13},{10,... | collective-permute-start | bytes 1990664 | tf_op jit(solution)/shard_map/ppermute | solution.py:559
  265.9 42.1 %collective-permute-start = (bf16[72,4608]{1,0:T(8,128)(2,1)}, bf16[72,4608]{1,0:T(8,128)(2,1)S(1)}, u32[]{:S(2)}, u32[]{:S(2)}) collective-permute-start(bf16[72,4608]{1,0:T(8,128)(2,1)} %get-tuple-element.24.refs_0_), channel_id=1, source_target_pairs={{0,2},{1,3},{2,0},{3,1},{4,6},{5,7},{6,4},{7,5},{8,10},{9,11},{10,... | collective-permute-start | bytes 1990664 | tf_op jit(solution)/shard_map/ppermute | solution.py:559
  279.6 45.0 %collective-permute-start.3 = (bf16[72,4608]{1,0:T(8,128)(2,1)}, bf16[72,4608]{1,0:T(8,128)(2,1)S(1)}, u32[]{:S(2)}, u32[]{:S(2)}) collective-permute-start(bf16[72,4608]{1,0:T(8,128)(2,1)} %get-tuple-element.25.refs_1_), channel_id=1, source_target_pairs={{0,4},{1,5},{2,6},{3,7},{4,0},{5,1},{6,2},{7,3},{8,12},{9,13},{10,... | collective-permute-start | bytes 1990664 | tf_op jit(solution)/shard_map/ppermute | solution.py:559
  281.0 43.9 %collective-permute-start.13 = (bf16[72,4608]{1,0:T(8,128)(2,1)}, bf16[72,4608]{1,0:T(8,128)(2,1)}, u32[]{:S(2)}, u32[]{:S(2)}) collective-permute-start(bf16[72,4608]{1,0:T(8,128)(2,1)} %get-tuple-element.25.refs_1_), channel_id=1, source_target_pairs={{0,2},{1,3},{2,0},{3,1},{4,6},{5,7},{6,4},{7,5},{8,10},{9,11},{10,... | collective-permute-start | bytes 1990664 | tf_op jit(solution)/shard_map/ppermute | solution.py:559
  293.8 31.4 %collective-permute-start.15 = (bf16[72,4608]{1,0:T(8,128)(2,1)}, bf16[72,4608]{1,0:T(8,128)(2,1)}, u32[]{:S(2)}, u32[]{:S(2)}) collective-permute-start(bf16[72,4608]{1,0:T(8,128)(2,1)} %get-tuple-element.24.refs_0_), channel_id=1, source_target_pairs={{0,4},{1,5},{2,6},{3,7},{4,0},{5,1},{6,2},{7,3},{8,12},{9,13},{10,... | collective-permute-start | bytes 1990664 | tf_op jit(solution)/shard_map/ppermute | solution.py:559
  295.3 30.1 %collective-permute-start.18 = (bf16[72,4608]{1,0:T(8,128)(2,1)S(1)}, bf16[72,4608]{1,0:T(8,128)(2,1)}, u32[]{:S(2)}, u32[]{:S(2)}) collective-permute-start(bf16[72,4608]{1,0:T(8,128)(2,1)S(1)} %collective-permute-done.6.refs_4_), channel_id=1, source_target_pairs={{0,1},{1,0},{2,3},{3,2},{4,5},{5,4},{6,7},{7,6},{8,9},{9,8},{10,11... | collective-permute-start | bytes 1990664 | tf_op jit(solution)/shard_map/ppermute | solution.py:559
  308.0 17.7 %collective-permute-start.23 = (bf16[72,4608]{1,0:T(8,128)(2,1)S(1)}, bf16[72,4608]{1,0:T(8,128)(2,1)}, u32[]{:S(2)}, u32[]{:S(2)}) collective-permute-start(bf16[72,4608]{1,0:T(8,128)(2,1)S(1)} %collective-permute-done.9.refs_7_), channel_id=1, source_target_pairs={{0,1},{1,0},{2,3},{3,2},{4,5},{5,4},{6,7},{7,6},{8,9},{9,8},{10,11... | collective-permute-start | bytes 1990664 | tf_op jit(solution)/shard_map/ppermute | solution.py:559
  325.4 10.8 %collective-permute-start.17 = (bf16[72,4608]{1,0:T(8,128)(2,1)S(1)}, bf16[72,4608]{1,0:T(8,128)(2,1)}, u32[]{:S(2)}, u32[]{:S(2)}) collective-permute-start(bf16[72,4608]{1,0:T(8,128)(2,1)S(1)} %collective-permute-done.3.refs_3_), channel_id=1, source_target_pairs={{0,1},{1,0},{2,3},{3,2},{4,5},{5,4},{6,7},{7,6},{8,9},{9,8},{10,11... | collective-permute-start | bytes 1990664 | tf_op jit(solution)/shard_map/ppermute | solution.py:559
  325.7 11.2 %collective-permute-start.14 = (bf16[72,4608]{1,0:T(8,128)(2,1)}, bf16[72,4608]{1,0:T(8,128)(2,1)}, u32[]{:S(2)}, u32[]{:S(2)}) collective-permute-start(bf16[72,4608]{1,0:T(8,128)(2,1)} %collective-permute-done.13.refs_1_), channel_id=1, source_target_pairs={{0,1},{1,0},{2,3},{3,2},{4,5},{5,4},{6,7},{7,6},{8,9},{9,8},{10,11... | collective-permute-start | bytes 1990664 | tf_op jit(solution)/shard_map/ppermute | solution.py:559
  332.7 18.0 %collective-permute-start.10 = (bf16[72,4608]{1,0:T(8,128)(2,1)S(1)}, bf16[72,4608]{1,0:T(8,128)(2,1)}, u32[]{:S(2)}, u32[]{:S(2)}) collective-permute-start(bf16[72,4608]{1,0:T(8,128)(2,1)S(1)} %collective-permute-done.9.refs_7_), channel_id=1, source_target_pairs={{0,2},{1,3},{2,0},{3,1},{4,6},{5,7},{6,4},{7,5},{8,10},{9,11},{10,... | collective-permute-start | bytes 1990664 | tf_op jit(solution)/shard_map/ppermute | solution.py:559
  334.2 17.9 %collective-permute-start.7 = (bf16[72,4608]{1,0:T(8,128)(2,1)S(1)}, bf16[72,4608]{1,0:T(8,128)(2,1)}, u32[]{:S(2)}, u32[]{:S(2)}) collective-permute-start(bf16[72,4608]{1,0:T(8,128)(2,1)S(1)} %collective-permute-done.6.refs_4_), channel_id=1, source_target_pairs={{0,4},{1,5},{2,6},{3,7},{4,0},{5,1},{6,2},{7,3},{8,12},{9,13},{10,... | collective-permute-start | bytes 1990664 | tf_op jit(solution)/shard_map/ppermute | solution.py:559
  335.8 29.5 %collective-permute-start.1 = (bf16[72,4608]{1,0:T(8,128)(2,1)S(1)}, bf16[72,4608]{1,0:T(8,128)(2,1)}, u32[]{:S(2)}, u32[]{:S(2)}) collective-permute-start(bf16[72,4608]{1,0:T(8,128)(2,1)S(1)} %collective-permute-done.refs_0_), channel_id=1, source_target_pairs={{0,4},{1,5},{2,6},{3,7},{4,0},{5,1},{6,2},{7,3},{8,12},{9,13},{10,... | collective-permute-start | bytes 1990664 | tf_op jit(solution)/shard_map/ppermute | solution.py:559
  336.2 29.1 %collective-permute-start.4 = (bf16[72,4608]{1,0:T(8,128)(2,1)S(1)}, bf16[72,4608]{1,0:T(8,128)(2,1)}, u32[]{:S(2)}, u32[]{:S(2)}) collective-permute-start(bf16[72,4608]{1,0:T(8,128)(2,1)S(1)} %collective-permute-done.3.refs_3_), channel_id=1, source_target_pairs={{0,2},{1,3},{2,0},{3,1},{4,6},{5,7},{6,4},{7,5},{8,10},{9,11},{10,... | collective-permute-start | bytes 1990664 | tf_op jit(solution)/shard_map/ppermute | solution.py:559
  336.8 29.0 %collective-permute-start.16 = (bf16[72,4608]{1,0:T(8,128)(2,1)}, bf16[72,4608]{1,0:T(8,128)(2,1)S(1)}, u32[]{:S(2)}, u32[]{:S(2)}) collective-permute-start(bf16[72,4608]{1,0:T(8,128)(2,1)} %collective-permute-done.15.refs_2_), channel_id=1, source_target_pairs={{0,1},{1,0},{2,3},{3,2},{4,5},{5,4},{6,7},{7,6},{8,9},{9,8},{10,11... | collective-permute-start | bytes 1990664 | tf_op jit(solution)/shard_map/ppermute | solution.py:559
  350.7 27.2 %collective-permute-start.11 = (bf16[72,4608]{1,0:T(8,128)(2,1)}, bf16[72,4608]{1,0:T(8,128)(2,1)S(1)}, u32[]{:S(2)}, u32[]{:S(2)}) collective-permute-start(bf16[72,4608]{1,0:T(8,128)(2,1)} %collective-permute-done.10.refs_3_), channel_id=1, source_target_pairs={{0,1},{1,0},{2,3},{3,2},{4,5},{5,4},{6,7},{7,6},{8,9},{9,8},{10,11... | collective-permute-start | bytes 1990664 | tf_op jit(solution)/shard_map/ppermute | solution.py:559
  352.1 25.8 %collective-permute-start.8 = (bf16[72,4608]{1,0:T(8,128)(2,1)}, bf16[72,4608]{1,0:T(8,128)(2,1)S(1)}, u32[]{:S(2)}, u32[]{:S(2)}) collective-permute-start(bf16[72,4608]{1,0:T(8,128)(2,1)} %collective-permute-done.7.refs_2_), channel_id=1, source_target_pairs={{0,1},{1,0},{2,3},{3,2},{4,5},{5,4},{6,7},{7,6},{8,9},{9,8},{10,11... | collective-permute-start | bytes 1990664 | tf_op jit(solution)/shard_map/ppermute | solution.py:559
  365.3 12.6 %collective-permute-start.2 = (bf16[72,4608]{1,0:T(8,128)(2,1)}, bf16[72,4608]{1,0:T(8,128)(2,1)S(1)}, u32[]{:S(2)}, u32[]{:S(2)}) collective-permute-start(bf16[72,4608]{1,0:T(8,128)(2,1)} %collective-permute-done.1.refs_0_), channel_id=1, source_target_pairs={{0,1},{1,0},{2,3},{3,2},{4,5},{5,4},{6,7},{7,6},{8,9},{9,8},{10,11... | collective-permute-start | bytes 1990664 | tf_op jit(solution)/shard_map/ppermute | solution.py:559
  365.3 12.6 %collective-permute-start.5 = (bf16[72,4608]{1,0:T(8,128)(2,1)}, bf16[72,4608]{1,0:T(8,128)(2,1)S(1)}, u32[]{:S(2)}, u32[]{:S(2)}) collective-permute-start(bf16[72,4608]{1,0:T(8,128)(2,1)} %collective-permute-done.4.refs_1_), channel_id=1, source_target_pairs={{0,1},{1,0},{2,3},{3,2},{4,5},{5,4},{6,7},{7,6},{8,9},{9,8},{10,11... | collective-permute-start | bytes 1990664 | tf_op jit(solution)/shard_map/ppermute | solution.py:559
  (18 other events, 221.7 us)
